TPU v7x, 32 devices: a whole 2x2x4 slice. The times are simulated.
32 devices in a mesh: gx: 4 (over z), gy: 4 (over x, core), gz: 2 (over y).
Axes of the slice: x: 2, y: 2, z: 4, core: 2. Of those that a mesh axis runs over, the one named last changes fastest.
Arguments:
- krylov_basis: float32 [60, 16, 32, 256], P(None, 'gx', 'gy', 'gz'), may hold values from -6 to 6
- schur_vectors: float32 [60, 20], replicated, may hold values from -1 to 1, as said below
- next_vector: float32 [16, 32, 256], P('gx', 'gy', 'gz'), may hold values from -10 to 10
- diag_shift: float32 [16, 32, 256], P('gx', 'gy', 'gz'), may hold values from 0.25 to 2
- velocity: float32 [3, 16, 32, 256], P(None, 'gx', 'gy', 'gz'), may hold values from -1 to 1
Outputs:
- new_basis: float32 [24, 16, 32, 256], P(None, 'gx', 'gy', 'gz')
- hessenberg: float32 [24, 3], replicated
Inputs may be any that keep to these rules, and one draw needn't show every extreme that they name: `schur_vectors`: the columns are orthonormal.
All inputs are finite; a program needn't handle non-finite values.
Results may differ from a plain program's by a relative error of at most 0.0003.
Values sent between devices are 32-bit elements; how exact they have to be, the bound alone decides.
A program may use at most 64 MiB of HBM per device.

v0:
```python
import functools

import jax
import jax.numpy as jnp
from jax import lax
from jax.experimental import pallas as pl
from jax.experimental.pallas import tpu as pltpu
from jax.sharding import PartitionSpec as P

KEEP = 20
EXPAND = 3
ROWS = 24
LANES = 128
UNIT = 16
DIRECT = 64
AXES = ("gx", "gy", "gz")


def partner_steps(phase, sizes):
    xs = range(1, sizes[0]) if phase else ()
    steps = [(dx, 0, 0) for dx in xs] if phase == 1 else [
        (dx, dy, dz) for dx in tuple(reversed(xs)) + (0,)
        for dy in range(sizes[1]) for dz in range(sizes[2])]
    return [step for step in steps if step != (0, 0, 0)]


def body(
    sizes, cells,
    kry_hbm, schur_hbm, w_hbm, diag_hbm, vel_hbm,
    out, hess,
    schur, w_ref, diag, vel, kry, image, xr, yr, zr, ypack, zpack, xh, yh, zh, xs, ys, zs,
    gsend, grecv0, grecv1, rsend, rrecv0, rrecv1, mid,
    load_sem, halo_send, halo_recv, gsem_s0, gsem_r0, gsem_s1, gsem_r1,
    rsem_s0, rsem_r0, rsem_s1, rsem_r1, ready,
):
    place = tuple(lax.axis_index(a) for a in AXES)
    basis = kry.shape[0]
    bx, by, bz = w_ref.shape
    loads = [
        pltpu.make_async_copy(source, target, load_sem.at[k])
        for k, (source, target) in enumerate((
            (w_hbm, w_ref), (schur_hbm, schur), (kry_hbm, kry), (diag_hbm, diag), (vel_hbm, vel)))
    ]
    for copy in loads:
        copy.start()
    direct = sizes[0] * sizes[1] * sizes[2] <= DIRECT
    shifted = [[lax.rem(place[d] + k, sizes[d]) for k in range(sizes[d])] for d in range(3)]

    def partners(phase):
        return [tuple(shifted[d][step[d]] for d in range(3))
                for step in partner_steps(phase, sizes)]


    for ref in (xr, yr, zr, xs, ys, zs):
        ref[...] = jnp.zeros_like(ref)

    barrier = pltpu.get_barrier_semaphore()
    for to in partners(0) + partners(1):
        pl.semaphore_signal(
            barrier, inc=1, device_id=to, device_id_type=pl.DeviceIdType.MESH)
    pl.semaphore_wait(barrier, len(partners(0)) + len(partners(1)))

    def halo_copies(kind, sources, targets):
        found = []
        for d in range(3):
            for side in (0, 1):
                at = (kind * 3 + d) * 2 + side
                to = list(place)
                to[d] = place[d] + (1 if side == 0 else -1)
                can_send = place[d] < sizes[d] - 1 if side == 0 else place[d] > 0
                can_recv = place[d] > 0 if side == 0 else place[d] < sizes[d] - 1
                found.append((
                    pltpu.make_async_remote_copy(
                        src_ref=sources[d][side], dst_ref=targets[d][side],
                        send_sem=halo_send.at[at], recv_sem=halo_recv.at[at],
                        device_id=tuple(to), device_id_type=pl.DeviceIdType.MESH,
                    ), can_send, can_recv))
        return found

    def halo_start(copies):
        for copy, can_send, _ in copies:
            pl.when(can_send)(copy.start)

    def halo_wait(copies):
        for copy, _, can_recv in copies:
            pl.when(can_recv)(copy.wait_recv)

    def halo_finish(copies):
        for copy, can_send, _ in copies:
            pl.when(can_send)(copy.wait_send)

    def field_copies(kind, ref):
        return halo_copies(
            kind,
            ((ref.at[bx - 1], ref.at[0]), (ref, ref), (ref, ref)),
            tuple((r.at[kind, 0], r.at[kind, 1]) for r in (xs, ys, zs)),
        )

    def exchange(send, slots, sem_s, sem_r, phase):
        for at, to in enumerate(partners(phase)):
            pltpu.make_async_remote_copy(
                src_ref=send, dst_ref=slots.at[at], send_sem=sem_s, recv_sem=sem_r,
                device_id=to, device_id_type=pl.DeviceIdType.MESH,
            ).start()
        pending.append(pltpu.make_async_copy(slots, slots, sem_s))
        return pltpu.make_async_copy(slots, slots, sem_r)

    def gather_sum(arrival, own, slots):
        arrival.wait()
        terms = [own] + [slots[k] for k in range(slots.shape[0])]
        while len(terms) > 1:
            terms = [sum(terms[k + 1:k + 2], terms[k]) for k in range(0, len(terms), 2)]
        return terms[0]

    pending = []

    def finish_sends():
        while pending:
            pending.pop().wait()

    def row_start(k, rowform):
        rsend[k] = rowform
        return exchange(rsend.at[k], rrecv0.at[k], rsem_s0.at[k], rsem_r0.at[k],
                        2 if direct else 0)

    def row_end(k, rowform, arrival):
        rowform = gather_sum(arrival, rowform, rrecv0.at[k])
        if not direct:
            mid[k] = rowform
            arrival = exchange(mid.at[k], rrecv1.at[k], rsem_s1.at[k], rsem_r1.at[k], 1)
            rowform = gather_sum(arrival, rowform, rrecv1.at[k])
        return rowform * (1.0 / cells)

    lane3 = lax.broadcasted_iota(jnp.int32, (by, bz), 1)
    row3 = lax.broadcasted_iota(jnp.int32, (by, bz), 0)

    def stencil(v, x_before, x_after, y_before, y_after, z_before, z_after):
        res = []
        for x in range(bx):
            here = v[x]
            xb = v[x - 1] if x > 0 else x_before
            xa = v[x + 1] if x < bx - 1 else x_after
            yb = jnp.where(row3 == 0, y_before[x], pltpu.roll(here, 1, 0))
            ya = jnp.where(row3 == by - 1, y_after[x], pltpu.roll(here, by - 1, 0))
            zb = jnp.where(lane3 == 0, z_before[x], pltpu.roll(here, 1, 1))
            za = jnp.where(lane3 == bz - 1, z_after[x], pltpu.roll(here, bz - 1, 1))
            neighbours = xa + xb + ya + yb + za + zb
            flow = (vel[0, x] * (xa - xb) + vel[1, x] * (ya - yb) + vel[2, x] * (za - zb))
            res.append((6.0 + diag[x]) * here - neighbours + 0.5 * flow)
        return res

    def dots(v, count, first=0):
        parts = []
        for i in range(ROWS):
            if first <= i < count:
                total = out[i, 0] * v[0]
                for x in range(1, bx):
                    total = total + out[i, x] * v[x]
            elif i == ROWS - 1:
                total = v[0] * v[0]
                for x in range(1, bx):
                    total = total + v[x] * v[x]
            else:
                total = None
            parts.append(jnp.zeros((1, bz), jnp.float32) if total is None
                         else jnp.sum(total, axis=0, keepdims=True))
        return jnp.sum(jnp.concatenate(parts, axis=0), axis=1, keepdims=True)

    halo_w = field_copies(0, w_ref)
    loads[0].wait()
    halo_start(halo_w)
    if direct:
        for to in partners(1):
            pl.semaphore_signal(
                ready, inc=1, device_id=to, device_id_type=pl.DeviceIdType.MESH)

    out[KEEP + 1:ROWS] = jnp.zeros((ROWS - KEEP - 1, bx, by, bz), jnp.float32)
    out[KEEP] = w_ref[...]
    loads[1].wait()
    loads[2].wait()
    wide, deep = 5, 4
    for first in range(0, KEEP, wide):
        def step(at, sums, first=first):
            sums = list(sums)
            for k in range(deep):
                i = at * deep + k
                for x in range(bx):
                    tile = kry[i, x]
                    for j in range(wide):
                        sums[j * bx + x] = sums[j * bx + x] + schur[first + j, i] * tile
            return tuple(sums)
        sums = lax.fori_loop(
            0, basis // deep, step,
            tuple(jnp.zeros((by, bz), jnp.float32) for _ in range(wide * bx)))
        for j in range(wide):
            for x in range(bx):
                out[first + j, x] = sums[j * bx + x]

    row = lax.broadcasted_iota(jnp.int32, (ROWS, LANES), 0)
    lane = lax.broadcasted_iota(jnp.int32, (ROWS, LANES), 1)
    lane1 = lax.broadcasted_iota(jnp.int32, (1, LANES), 1)
    row1 = lax.broadcasted_iota(jnp.int32, (ROWS, 1), 0)

    gram = jnp.zeros((ROWS, LANES), jnp.float32)
    for j in range(KEEP + 1):
        col = dots([out[j, x] for x in range(bx)], KEEP + 1, j // 8 * 8)
        gram = jnp.where((lane == j) & (row < KEEP + 1), col, gram)
    lane8 = lax.broadcasted_iota(jnp.int32, (8, LANES), 1)
    own8 = lane8 // UNIT == lax.broadcasted_iota(jnp.int32, (8, LANES), 0)

    def spread(value):
        for shift in (UNIT, 2 * UNIT, 4 * UNIT):
            value = value + pltpu.roll(value, shift, 1)
        return value

    units = (
        gram[16:24],
        gram[8:16],
        jnp.where(lane8 < 8, gram[0:8], pltpu.roll(gram[16:24], LANES - 8, 1)),
    )
    packed = jnp.concatenate([
        jnp.sum(jnp.where(own8, spread(jnp.where(lane8 < UNIT, unit, 0.0)), 0.0),
                axis=0, keepdims=True)
        for unit in units], axis=0)
    gsend[0] = packed
    if direct:
        pl.semaphore_wait(ready, sizes[0] - 1)
    arrival0 = exchange(gsend.at[0], grecv1, gsem_s1, gsem_r1, 2 if direct else 1)

    loads[3].wait()
    loads[4].wait()
    halo_wait(halo_w)
    applied = stencil(
        [w_ref[x] for x in range(bx)], xs[0, 0], xs[0, 1],
        [ys[0, 0, x, by - 1:by, :] for x in range(bx)],
        [ys[0, 1, x, 0:1, :] for x in range(bx)],
        [zs[0, 0, x, :, bz - 1:bz] for x in range(bx)],
        [zs[0, 1, x, :, 0:1] for x in range(bx)],
    )
    for x in range(bx):
        image[0, x] = applied[x]
    ownrow = jnp.sum(jnp.where(row == lane, dots(applied, KEEP + 1), 0.0),
                     axis=0, keepdims=True)
    copies = row_start(0, ownrow)
    halo_a = field_copies(1, image.at[0])
    halo_start(halo_a)

    for side, (near, edge) in enumerate(((by - 1, bz - 1), (0, 0))):
        for i in range(KEEP):
            ypack[side, i] = out[i, :, near, :]
        for x in range(bx):
            face = jnp.zeros((by, bz), jnp.float32)
            for i in range(KEEP):
                face = jnp.where(
                    lane3 == i, pltpu.roll(out[i, x], (i - edge) % bz, 1), face)
            zpack[side, x] = face
    halo_r = halo_copies(
        3,
        ((out.at[0:KEEP, bx - 1], out.at[0:KEEP, 0]), (ypack.at[0], ypack.at[1]),
         (zpack.at[0], zpack.at[1])),
        tuple((r.at[0], r.at[1]) for r in (xr, yr, zr)),
    )
    halo_start(halo_r)

    packed = gather_sum(arrival0, packed, grecv1)
    if not direct:
        gsend[1] = packed
        arrival1 = exchange(gsend.at[1], grecv0, gsem_s0, gsem_r0, 0)
        packed = gather_sum(arrival1, packed, grecv0)
    packed = packed * (1.0 / cells)
    units = [
        jnp.where(lane8 < UNIT,
                  spread(jnp.where(own8, jnp.broadcast_to(packed[u:u + 1], (8, LANES)), 0.0)),
                  0.0)
        for u in range(3)]
    corner = pltpu.roll(jnp.where(lane8 >= 8, units[2], 0.0), 8, 1)
    below = jnp.concatenate(
        [jnp.zeros((8, LANES), jnp.float32), jnp.where(lane8 < 8, units[1], 0.0), units[0],
         jnp.zeros((LANES - ROWS, LANES), jnp.float32)], axis=0)
    gram = jnp.concatenate(
        [jnp.where(lane8 < 8, units[2], 0.0), units[1], units[0] + corner], axis=0)
    gram = gram + below.T[0:ROWS]
    gram = jnp.where((lane < KEEP + 1) & (row < KEEP + 1), gram, 0.0)
    norm_sq = jnp.sum(
        jnp.sum(jnp.where((lane == KEEP) & (row == KEEP), gram, 0.0), axis=1, keepdims=True),
        axis=0, keepdims=True)
    scale = 1.0 / jnp.maximum(jnp.sqrt(norm_sq), 0.5)
    gram = gram * jnp.where(row == KEEP, scale, 1.0) * jnp.where(lane == KEEP, scale, 1.0)
    for x in range(bx):
        out[KEEP, x] = w_ref[x] * scale
    applied = [tile * scale for tile in applied]
    rowform = row_end(0, ownrow, copies)
    rowform = rowform * scale * jnp.where((lane1 == KEEP) | (lane1 == ROWS - 1), scale, 1.0)

    halo_wait(halo_r)
    for side in (0, 1):
        near_row, near_lane = (by - 1, bz - 1) if side == 0 else (0, 0)
        xh[side, 0] = xs[0, side] * scale
        for x in range(bx):
            yh[side, 0, x:x + 1] = ys[0, side, x, near_row:near_row + 1, :] * scale
            zh[side, x] = jnp.where(
                lane3 == KEEP, zs[0, side, x, :, near_lane:near_lane + 1] * scale, zr[side, x])
    halos = {1: halo_a}
    done = [halo_w, halo_r, halo_a]
    hcols = []
    for k in range(EXPAND):
        count = KEEP + 1 + k
        if k > 0:
            rowform = jnp.sum(jnp.where(row == lane, dots(applied, count), 0.0),
                              axis=0, keepdims=True)
            earlier = pending[:]
            pending.clear()
            arrival = row_start(k, rowform)
            for copy in earlier:
                copy.wait()
            for copies in done:
                halo_finish(copies)
            done = []
            rowform = row_end(k, rowform, arrival)
        c_row = jnp.where(lane1 < count, rowform, 0.0)
        twice = jnp.where(row == lane, 2.0, 0.0) - gram
        t_col = jnp.sum(twice * c_row, axis=1, keepdims=True)
        weights = jnp.broadcast_to(t_col, (ROWS, LANES))
        t_row = jnp.sum(jnp.where(row == lane, weights, 0.0), axis=0, keepdims=True)
        gt_row = jnp.sum(gram * weights, axis=0, keepdims=True)
        length_sq = jnp.sum(
            jnp.where(lane1 == ROWS - 1, rowform, t_row * (gt_row - 2.0 * c_row)),
            axis=1, keepdims=True)
        length_sq = jnp.maximum(length_sq, 0.0)
        length = jnp.sqrt(length_sq)
        inverse = 1.0 / jnp.maximum(length, 0.5)
        hcols.append(jnp.where(lane1 == count, length, t_row))
        newest = list(applied)
        for i in range(count):
            weight = jnp.broadcast_to(weights[i:i + 1, :], (by, bz))
            for x in range(bx):
                newest[x] = newest[x] - weight * out[i, x]
        newest = [tile * inverse for tile in newest]
        for x in range(bx):
            out[count, x] = newest[x]
        if k == EXPAND - 1:
            break
        halo_wait(halos[k + 1])
        sides = []
        for side in (0, 1):
            near_row, near_lane = (by - 1, bz - 1) if side == 0 else (0, 0)
            factor = scale if k == 0 else 1.0
            x_part = xs[k + 1, side] * factor
            y_part = [ys[k + 1, side, x, near_row:near_row + 1, :] * factor for x in range(bx)]
            y_part = jnp.concatenate(y_part, axis=0)
            for i in range(count):
                weight = weights[i:i + 1, :]
                if i < KEEP:
                    x_part = x_part - weight * xr[side, i]
                    y_part = y_part - weight * yr[side, i]
                else:
                    x_part = x_part - weight * xh[side, i - KEEP]
                    y_part = y_part - weight * yh[side, i - KEEP]
            x_part = x_part * inverse
            y_part = y_part * inverse
            z_part = []
            for x in range(bx):
                column = (zs[k + 1, side, x, :, near_lane:near_lane + 1] * factor
                          - jnp.sum(zh[side, x] * t_row, axis=1, keepdims=True)) * inverse
                z_part.append(column)
                if k + 1 < EXPAND - 1:
                    zh[side, x] = jnp.where(lane3 == count, column, zh[side, x])
            xh[side, count - KEEP] = x_part
            yh[side, count - KEEP] = y_part
            sides.append((x_part, [y_part[x:x + 1] for x in range(bx)], z_part))
        applied = stencil(newest, sides[0][0], sides[1][0], sides[0][1], sides[1][1],
                          sides[0][2], sides[1][2])
        if k + 1 < EXPAND - 1:
            for x in range(bx):
                image[1, x] = applied[x]
            halos[k + 2] = field_copies(k + 2, image.at[1])
            halo_start(halos[k + 2])
            done.append(halos[k + 2])
        e_row = t_row - c_row
        e_col = jnp.sum(jnp.where(row == lane, e_row, 0.0), axis=1, keepdims=True)
        cross_col = (e_col - jnp.sum(gram * e_row, axis=1, keepdims=True)) * inverse
        cross_row = (e_row - jnp.sum(gram * e_col, axis=0, keepdims=True)) * inverse
        corner = length_sq * inverse * inverse
        gram = jnp.where(row == count, cross_row, jnp.where(lane == count, cross_col, gram))
        gram = jnp.where((row == count) & (lane == count), corner, gram)

    for k in range(EXPAND):
        hess[k:k + 1] = hcols[k % len(hcols)]
    for copies in done:
        halo_finish(copies)
    finish_sends()


def per_device(krylov_basis, schur_vectors, next_vector, diag_shift, velocity):
    sizes = tuple(lax.axis_size(a) for a in AXES)
    block = next_vector.shape
    bx, by, bz = block
    cells = float(bx * by * bz * sizes[0] * sizes[1] * sizes[2])
    n0, n1 = sizes[1] * sizes[2], sizes[0]
    nrow = n0 * n1 if n0 * n1 <= DIRECT else n0
    nline = n0 * n1 if n0 * n1 <= DIRECT else n1
    f32 = jnp.float32
    vmem = pl.BlockSpec(memory_space=pltpu.VMEM)
    dma = pltpu.SemaphoreType.DMA
    vectors, columns = pl.pallas_call(
        functools.partial(body, sizes, cells),
        out_shape=(
            pltpu.VMEM((ROWS,) + block, f32),
            pltpu.VMEM((8, LANES), f32),
        ),
        in_specs=[
            pl.BlockSpec(memory_space=pl.ANY) for _ in range(5)
        ],
        out_specs=(vmem, vmem),
        scratch_shapes=[
            pltpu.SMEM(schur_vectors.shape[::-1], f32),
            pltpu.VMEM(block, f32),
            pltpu.VMEM(block, f32),
            pltpu.VMEM((3,) + block, f32),
            pltpu.VMEM(krylov_basis.shape, f32),
            pltpu.VMEM((2,) + block, f32),
            pltpu.VMEM((2, KEEP, by, bz), f32),
            pltpu.VMEM((2, KEEP, bx, bz), f32),
            pltpu.VMEM((2,) + block, f32),
            pltpu.VMEM((2, KEEP, bx, bz), f32),
            pltpu.VMEM((2,) + block, f32),
            pltpu.VMEM((2, EXPAND, by, bz), f32),
            pltpu.VMEM((2, EXPAND, bx, bz), f32),
            pltpu.VMEM((2,) + block, f32),
            pltpu.VMEM((EXPAND, 2, by, bz), f32),
            pltpu.VMEM((EXPAND, 2) + block, f32),
            pltpu.VMEM((EXPAND, 2) + block, f32),
            pltpu.VMEM((2, 3, LANES), f32),
            pltpu.VMEM((n0 - 1, 3, LANES), f32),
            pltpu.VMEM((nline - 1, 3, LANES), f32),
            pltpu.VMEM((EXPAND, 1, LANES), f32),
            pltpu.VMEM((EXPAND, nrow - 1, 1, LANES), f32),
            pltpu.VMEM((EXPAND, n1 - 1, 1, LANES), f32),
            pltpu.VMEM((EXPAND, 1, LANES), f32),
            dma((5,)), dma((24,)), dma((24,)),
            dma, dma, dma, dma,
            dma((EXPAND,)), dma((EXPAND,)), dma((EXPAND,)), dma((EXPAND,)),
            pltpu.SemaphoreType.REGULAR,
        ],
        compiler_params=pltpu.CompilerParams(collective_id=0, has_side_effects=True),
    )(krylov_basis, schur_vectors.T, next_vector, diag_shift, velocity)
    return vectors, columns[0:EXPAND, 0:ROWS].T


def solution(mesh):
    in_specs = (
        P(None, "gx", "gy", "gz"),
        P(),
        P("gx", "gy", "gz"),
        P("gx", "gy", "gz"),
        P(None, "gx", "gy", "gz"),
    )
    out_specs = (P(None, "gx", "gy", "gz"), P())
    return jax.shard_map(
        per_device, mesh=mesh, in_specs=in_specs, out_specs=out_specs, check_vma=False
    )
```

profile of v0, /device:TPU:0, one launch (start us, length us, event | category | flops | bytes accessed | tf_op | source)
XLA Modules:
  0.0 26.4 jit_solution(16378273145687143570)
XLA Ops:
  0.6 24.4 %shard_map.68 = (f32[24,4,8,128]{3,2,1,0:T(8,128)S(1)}, f32[8,128]{1,0:T(8,128)S(1)}) custom-call(f32[60,4,8,128]{3,2,1,0:T(8,128)} %kry_hbm.1, f32[20,60]{1,0:T(8,128)} %bitcast.3, f32[4,8,128]{2,1,0:T(8,128)} %w_hbm.1, f32[4,8,128]{2,1,0:T(8,128)} %diag_hbm.1, f32[3,4,8,128]{3,2,1,0:T(8,128)} %vel_hbm.1), custom_call_target="tpu_custom_call" | custom-call | tf_op jit(solution)/shard_map/pallas_call | solution.py:405
  25.0 0.7 %copy.8 = f32[24,4,8,128]{3,2,1,0:T(8,128)} copy(f32[24,4,8,128]{3,2,1,0:T(8,128)S(1)} %get-tuple-element.6) | data formatting | bytes 786432
  25.8 0.6 %slice_bitcast_fusion = f32[24,3]{0,1:T(4,128)} fusion(f32[8,128]{1,0:T(8,128)S(1)} %get-tuple-element.5), kind=kLoop, calls=%fused_computation | loop fusion | bytes 576 | tf_op jit(solution)/shard_map/transpose | solution.py:447
where the time goes:
time: 26.5 us; the launch traced here: 26.4 us
  Pallas kernels  24.4 us (92%)
  local copies, waits for them, and re-layouts  1.33 us (5%)
  between operations  0.64 us (2%)
    pallas_call x1, Pallas kernels, per_device(): pl.pallas_call(functools.partial(body, sizes, cells), out_shape=(pltpu.VM...  24.4 us
    unnamed x1, local copies, waits for them, and re-layouts  0.75 us
    transpose x1, local copies, waits for them, and re-layouts, per_device(): return (vectors, columns[0:EXPAND, 0:ROWS].T)  0.58 us

commit v1 on v0

--- a/solution.py
+++ b/solution.py
@@ -29,9 +29,10 @@
     kry_hbm, schur_hbm, w_hbm, diag_hbm, vel_hbm,
     out, hess,
     schur, w_ref, diag, vel, kry, image, xr, yr, zr, ypack, zpack, xh, yh, zh, xs, ys, zs,
-    gsend, grecv0, grecv1, rsend, rrecv0, rrecv1, mid,
-    load_sem, halo_send, halo_recv, gsem_s0, gsem_r0, gsem_s1, gsem_r1,
-    rsem_s0, rsem_r0, rsem_s1, rsem_r1, ready,
+    gsend, grecv0, grecv1,
+    rsend, rrecv0, rmid, rrecv1, msend, mrecv0, mmid, mrecv1, lsend, lrecv0, lmid, lrecv1,
+    ubuf, abuf,
+    load_sem, halo_send, halo_recv, gsem_s0, gsem_r0, gsem_s1, gsem_r1, sums_sem, ready,
 ):
     place = tuple(lax.axis_index(a) for a in AXES)
     basis = kry.shape[0]
@@ -118,18 +119,22 @@
         while pending:
             pending.pop().wait()
 
-    def row_start(k, rowform):
-        rsend[k] = rowform
-        return exchange(rsend.at[k], rrecv0.at[k], rsem_s0.at[k], rsem_r0.at[k],
-                        2 if direct else 0)
-
-    def row_end(k, rowform, arrival):
-        rowform = gather_sum(arrival, rowform, rrecv0.at[k])
+    groups = (
+        (rsend, rrecv0, rmid, rrecv1), (msend, mrecv0, mmid, mrecv1), (lsend, lrecv0, lmid, lrecv1))
+
+    def total_start(k, value):
+        send, first = groups[k][:2]
+        send[...] = value
+        return exchange(send, first, sums_sem.at[k, 0], sums_sem.at[k, 1], 2 if direct else 0)
+
+    def total_end(k, value, arrival):
+        first, between, second = groups[k][1:]
+        value = gather_sum(arrival, value, first)
         if not direct:
-            mid[k] = rowform
-            arrival = exchange(mid.at[k], rrecv1.at[k], rsem_s1.at[k], rsem_r1.at[k], 1)
-            rowform = gather_sum(arrival, rowform, rrecv1.at[k])
-        return rowform * (1.0 / cells)
+            between[...] = value
+            arrival = exchange(between, second, sums_sem.at[k, 2], sums_sem.at[k, 3], 1)
+            value = gather_sum(arrival, value, second)
+        return value * (1.0 / cells)
 
     lane3 = lax.broadcasted_iota(jnp.int32, (by, bz), 1)
     row3 = lax.broadcasted_iota(jnp.int32, (by, bz), 0)
@@ -149,22 +154,43 @@
             res.append((6.0 + diag[x]) * here - neighbours + 0.5 * flow)
         return res
 
-    def dots(v, count, first=0):
-        parts = []
-        for i in range(ROWS):
-            if first <= i < count:
-                total = out[i, 0] * v[0]
+    row8 = lax.broadcasted_iota(jnp.int32, (8, LANES), 0)
+
+    def fold(tiles):
+        for half in (4, 2, 1):
+            low = (row8 & half) == 0
+            tiles = [
+                jnp.where(low, tiles[k] + pltpu.roll(tiles[k], 8 - half, 0),
+                          tiles[k + half] + pltpu.roll(tiles[k + half], half, 0))
+                for k in range(half)]
+        return tiles[0]
+
+    def dots(v, fields):
+        groups = []
+        for first in range(0, ROWS, 8):
+            tiles = []
+            for k in range(first, first + 8):
+                field = fields[k] if k < len(fields) else None
+                if field is None:
+                    tiles.append(None)
+                    continue
+                total = field(0) * v[0]
                 for x in range(1, bx):
-                    total = total + out[i, x] * v[x]
-            elif i == ROWS - 1:
-                total = v[0] * v[0]
-                for x in range(1, bx):
-                    total = total + v[x] * v[x]
+                    total = total + field(x) * v[x]
+                if by > 8:
+                    total = sum(total[8 * t:8 * t + 8] for t in range(1, by // 8)) + total[0:8]
+                tiles.append(total)
+            if all(tile is None for tile in tiles):
+                groups.append(jnp.zeros((8, bz), jnp.float32))
             else:
-                total = None
-            parts.append(jnp.zeros((1, bz), jnp.float32) if total is None
-                         else jnp.sum(total, axis=0, keepdims=True))
-        return jnp.sum(jnp.concatenate(parts, axis=0), axis=1, keepdims=True)
+                groups.append(fold([
+                    jnp.zeros((8, bz), jnp.float32) if t is None else t for t in tiles]))
+        return jnp.sum(jnp.concatenate(groups, axis=0), axis=1, keepdims=True)
+
+    def of(ref, *at):
+        return lambda x: ref[at + (x,)]
+
+    basis_fields = [of(out, i) for i in range(ROWS)]
 
     halo_w = field_copies(0, w_ref)
     loads[0].wait()
@@ -196,55 +222,6 @@
             for x in range(bx):
                 out[first + j, x] = sums[j * bx + x]
 
-    row = lax.broadcasted_iota(jnp.int32, (ROWS, LANES), 0)
-    lane = lax.broadcasted_iota(jnp.int32, (ROWS, LANES), 1)
-    lane1 = lax.broadcasted_iota(jnp.int32, (1, LANES), 1)
-    row1 = lax.broadcasted_iota(jnp.int32, (ROWS, 1), 0)
-
-    gram = jnp.zeros((ROWS, LANES), jnp.float32)
-    for j in range(KEEP + 1):
-        col = dots([out[j, x] for x in range(bx)], KEEP + 1, j // 8 * 8)
-        gram = jnp.where((lane == j) & (row < KEEP + 1), col, gram)
-    lane8 = lax.broadcasted_iota(jnp.int32, (8, LANES), 1)
-    own8 = lane8 // UNIT == lax.broadcasted_iota(jnp.int32, (8, LANES), 0)
-
-    def spread(value):
-        for shift in (UNIT, 2 * UNIT, 4 * UNIT):
-            value = value + pltpu.roll(value, shift, 1)
-        return value
-
-    units = (
-        gram[16:24],
-        gram[8:16],
-        jnp.where(lane8 < 8, gram[0:8], pltpu.roll(gram[16:24], LANES - 8, 1)),
-    )
-    packed = jnp.concatenate([
-        jnp.sum(jnp.where(own8, spread(jnp.where(lane8 < UNIT, unit, 0.0)), 0.0),
-                axis=0, keepdims=True)
-        for unit in units], axis=0)
-    gsend[0] = packed
-    if direct:
-        pl.semaphore_wait(ready, sizes[0] - 1)
-    arrival0 = exchange(gsend.at[0], grecv1, gsem_s1, gsem_r1, 2 if direct else 1)
-
-    loads[3].wait()
-    loads[4].wait()
-    halo_wait(halo_w)
-    applied = stencil(
-        [w_ref[x] for x in range(bx)], xs[0, 0], xs[0, 1],
-        [ys[0, 0, x, by - 1:by, :] for x in range(bx)],
-        [ys[0, 1, x, 0:1, :] for x in range(bx)],
-        [zs[0, 0, x, :, bz - 1:bz] for x in range(bx)],
-        [zs[0, 1, x, :, 0:1] for x in range(bx)],
-    )
-    for x in range(bx):
-        image[0, x] = applied[x]
-    ownrow = jnp.sum(jnp.where(row == lane, dots(applied, KEEP + 1), 0.0),
-                     axis=0, keepdims=True)
-    copies = row_start(0, ownrow)
-    halo_a = field_copies(1, image.at[0])
-    halo_start(halo_a)
-
     for side, (near, edge) in enumerate(((by - 1, bz - 1), (0, 0))):
         for i in range(KEEP):
             ypack[side, i] = out[i, :, near, :]
@@ -261,6 +238,82 @@
         tuple((r.at[0], r.at[1]) for r in (xr, yr, zr)),
     )
     halo_start(halo_r)
+
+    row = lax.broadcasted_iota(jnp.int32, (ROWS, LANES), 0)
+    lane = lax.broadcasted_iota(jnp.int32, (ROWS, LANES), 1)
+    lane1 = lax.broadcasted_iota(jnp.int32, (1, LANES), 1)
+    row1 = lax.broadcasted_iota(jnp.int32, (ROWS, 1), 0)
+
+    def as_row(col, shift=0):
+        return jnp.sum(jnp.where(row + shift == lane, col, 0.0), axis=0, keepdims=True)
+
+    def as_col(values):
+        return jnp.sum(jnp.where(row == lane, values, 0.0), axis=1, keepdims=True)
+
+    gram = jnp.zeros((ROWS, LANES), jnp.float32)
+    for j in range(KEEP + 1):
+        col = dots([out[j, x] for x in range(bx)],
+                   [None] * (j // 8 * 8) + basis_fields[j // 8 * 8:KEEP + 1])
+        gram = jnp.where((lane == j) & (row < KEEP + 1), col, gram)
+    lane8 = lax.broadcasted_iota(jnp.int32, (8, LANES), 1)
+    own8 = lane8 // UNIT == lax.broadcasted_iota(jnp.int32, (8, LANES), 0)
+
+    def spread(value):
+        for shift in (UNIT, 2 * UNIT, 4 * UNIT):
+            value = value + pltpu.roll(value, shift, 1)
+        return value
+
+    units = (
+        gram[16:24],
+        gram[8:16],
+        jnp.where(lane8 < 8, gram[0:8], pltpu.roll(gram[16:24], LANES - 8, 1)),
+    )
+    packed = jnp.concatenate([
+        jnp.sum(jnp.where(own8, spread(jnp.where(lane8 < UNIT, unit, 0.0)), 0.0),
+                axis=0, keepdims=True)
+        for unit in units], axis=0)
+    gsend[0] = packed
+    if direct:
+        pl.semaphore_wait(ready, sizes[0] - 1)
+    arrival0 = exchange(gsend.at[0], grecv1, gsem_s1, gsem_r1, 2 if direct else 1)
+
+    loads[3].wait()
+    loads[4].wait()
+    halo_wait(halo_w)
+    applied = stencil(
+        [w_ref[x] for x in range(bx)], xs[0, 0], xs[0, 1],
+        [ys[0, 0, x, by - 1:by, :] for x in range(bx)],
+        [ys[0, 1, x, 0:1, :] for x in range(bx)],
+        [zs[0, 0, x, :, bz - 1:bz] for x in range(bx)],
+        [zs[0, 1, x, :, 0:1] for x in range(bx)],
+    )
+    for x in range(bx):
+        image[0, x] = applied[x]
+    ownrow = as_row(dots(applied, basis_fields[:KEEP + 1] + [None, None, of(image, 0)]))
+    row_arrival = total_start(0, ownrow)
+    halo_a = field_copies(1, image.at[0])
+    halo_start(halo_a)
+
+    halo_wait(halo_r)
+    for i in range(KEEP):
+        found = stencil(
+            [out[i, x] for x in range(bx)], xr[0, i], xr[1, i],
+            [yr[0, i, x:x + 1] for x in range(bx)], [yr[1, i, x:x + 1] for x in range(bx)],
+            [zr[0, x, :, i:i + 1] for x in range(bx)], [zr[1, x, :, i:i + 1] for x in range(bx)])
+        for x in range(bx):
+            ubuf[i, x] = found[x]
+    ufields = [of(ubuf, i) for i in range(KEEP)]
+    shares = [jnp.zeros((ROWS, LANES), jnp.float32) for _ in range(2)]
+    for j in range(KEEP):
+        v = [ubuf[j, x] for x in range(bx)]
+        cols = (dots(v, basis_fields[:KEEP] + [of(w_ref), of(image, 0)]),
+                dots(v, [None] * (j // 8 * 8) + ufields[j // 8 * 8:]))
+        shares = [jnp.where(lane == j, col, part) for col, part in zip(cols, shares)]
+    mixed = jnp.zeros((8, LANES), jnp.float32)
+    for k in range(6):
+        part = shares[k // 3][k % 3 * 8:k % 3 * 8 + 8]
+        mixed = mixed + (part if k == 0 else pltpu.roll(part, KEEP * k, 1))
+    mix_arrival = total_start(1, mixed)
 
     packed = gather_sum(arrival0, packed, grecv1)
     if not direct:
@@ -289,10 +342,9 @@
     for x in range(bx):
         out[KEEP, x] = w_ref[x] * scale
     applied = [tile * scale for tile in applied]
-    rowform = row_end(0, ownrow, copies)
+    rowform = total_end(0, ownrow, row_arrival)
     rowform = rowform * scale * jnp.where((lane1 == KEEP) | (lane1 == ROWS - 1), scale, 1.0)
 
-    halo_wait(halo_r)
     for side in (0, 1):
         near_row, near_lane = (by - 1, bz - 1) if side == 0 else (0, 0)
         xh[side, 0] = xs[0, side] * scale
@@ -300,94 +352,149 @@
             yh[side, 0, x:x + 1] = ys[0, side, x, near_row:near_row + 1, :] * scale
             zh[side, x] = jnp.where(
                 lane3 == KEEP, zs[0, side, x, :, near_lane:near_lane + 1] * scale, zr[side, x])
-    halos = {1: halo_a}
-    done = [halo_w, halo_r, halo_a]
+    for x in range(bx):
+        abuf[x] = applied[x]
     hcols = []
-    for k in range(EXPAND):
-        count = KEEP + 1 + k
-        if k > 0:
-            rowform = jnp.sum(jnp.where(row == lane, dots(applied, count), 0.0),
-                              axis=0, keepdims=True)
-            earlier = pending[:]
-            pending.clear()
-            arrival = row_start(k, rowform)
-            for copy in earlier:
-                copy.wait()
-            for copies in done:
-                halo_finish(copies)
-            done = []
-            rowform = row_end(k, rowform, arrival)
-        c_row = jnp.where(lane1 < count, rowform, 0.0)
+
+    def step(count, c_row, c_col, image_sq, gram):
         twice = jnp.where(row == lane, 2.0, 0.0) - gram
-        t_col = jnp.sum(twice * c_row, axis=1, keepdims=True)
+        if c_col is None:
+            t_col = jnp.sum(twice * c_row, axis=1, keepdims=True)
+            t_row = as_row(t_col)
+        else:
+            t_row = jnp.sum(twice * c_col, axis=0, keepdims=True)
+            t_col = as_col(t_row)
         weights = jnp.broadcast_to(t_col, (ROWS, LANES))
-        t_row = jnp.sum(jnp.where(row == lane, weights, 0.0), axis=0, keepdims=True)
         gt_row = jnp.sum(gram * weights, axis=0, keepdims=True)
-        length_sq = jnp.sum(
-            jnp.where(lane1 == ROWS - 1, rowform, t_row * (gt_row - 2.0 * c_row)),
-            axis=1, keepdims=True)
+        length_sq = image_sq + jnp.sum(t_row * (gt_row - 2.0 * c_row), axis=1, keepdims=True)
         length_sq = jnp.maximum(length_sq, 0.0)
         length = jnp.sqrt(length_sq)
         inverse = 1.0 / jnp.maximum(length, 0.5)
         hcols.append(jnp.where(lane1 == count, length, t_row))
-        newest = list(applied)
-        for i in range(count):
+        return t_row, t_col, weights, length_sq, inverse
+
+    def less(start, weights, fields):
+        for i, field in enumerate(fields):
             weight = jnp.broadcast_to(weights[i:i + 1, :], (by, bz))
-            for x in range(bx):
-                newest[x] = newest[x] - weight * out[i, x]
-        newest = [tile * inverse for tile in newest]
-        for x in range(bx):
-            out[count, x] = newest[x]
-        if k == EXPAND - 1:
-            break
-        halo_wait(halos[k + 1])
-        sides = []
-        for side in (0, 1):
-            near_row, near_lane = (by - 1, bz - 1) if side == 0 else (0, 0)
-            factor = scale if k == 0 else 1.0
-            x_part = xs[k + 1, side] * factor
-            y_part = [ys[k + 1, side, x, near_row:near_row + 1, :] * factor for x in range(bx)]
-            y_part = jnp.concatenate(y_part, axis=0)
-            for i in range(count):
-                weight = weights[i:i + 1, :]
-                if i < KEEP:
-                    x_part = x_part - weight * xr[side, i]
-                    y_part = y_part - weight * yr[side, i]
-                else:
-                    x_part = x_part - weight * xh[side, i - KEEP]
-                    y_part = y_part - weight * yh[side, i - KEEP]
-            x_part = x_part * inverse
-            y_part = y_part * inverse
-            z_part = []
-            for x in range(bx):
-                column = (zs[k + 1, side, x, :, near_lane:near_lane + 1] * factor
-                          - jnp.sum(zh[side, x] * t_row, axis=1, keepdims=True)) * inverse
-                z_part.append(column)
-                if k + 1 < EXPAND - 1:
-                    zh[side, x] = jnp.where(lane3 == count, column, zh[side, x])
-            xh[side, count - KEEP] = x_part
-            yh[side, count - KEEP] = y_part
-            sides.append((x_part, [y_part[x:x + 1] for x in range(bx)], z_part))
-        applied = stencil(newest, sides[0][0], sides[1][0], sides[0][1], sides[1][1],
-                          sides[0][2], sides[1][2])
-        if k + 1 < EXPAND - 1:
-            for x in range(bx):
-                image[1, x] = applied[x]
-            halos[k + 2] = field_copies(k + 2, image.at[1])
-            halo_start(halos[k + 2])
-            done.append(halos[k + 2])
+            start = [start[x] - weight * field(x) for x in range(bx)]
+        return start
+
+    def widen(gram, count, t_row, c_row, length_sq, inverse):
         e_row = t_row - c_row
-        e_col = jnp.sum(jnp.where(row == lane, e_row, 0.0), axis=1, keepdims=True)
+        e_col = as_col(e_row)
         cross_col = (e_col - jnp.sum(gram * e_row, axis=1, keepdims=True)) * inverse
         cross_row = (e_row - jnp.sum(gram * e_col, axis=0, keepdims=True)) * inverse
         corner = length_sq * inverse * inverse
         gram = jnp.where(row == count, cross_row, jnp.where(lane == count, cross_col, gram))
-        gram = jnp.where((row == count) & (lane == count), corner, gram)
+        return jnp.where((row == count) & (lane == count), corner, gram)
+
+    def pick(values, at):
+        return jnp.sum(jnp.where(lane1 == at, values, 0.0), axis=1, keepdims=True)
+
+    count = KEEP + 1
+    first_row = jnp.where(lane1 < count, rowform, 0.0)
+    image_sq = pick(rowform, ROWS - 1)
+    t_row, t_col, weights, length_sq, inverse = step(count, first_row, None, image_sq, gram)
+    newest = [tile * inverse for tile in less(applied, weights, basis_fields[:count])]
+    for x in range(bx):
+        out[count, x] = newest[x]
+    halo_wait(halo_a)
+    sides = []
+    for side in (0, 1):
+        near_row, near_lane = (by - 1, bz - 1) if side == 0 else (0, 0)
+        x_part = xs[1, side] * scale
+        y_part = [ys[1, side, x, near_row:near_row + 1, :] * scale for x in range(bx)]
+        y_part = jnp.concatenate(y_part, axis=0)
+        for i in range(count):
+            weight = weights[i:i + 1, :]
+            x_part = x_part - weight * (xr[side, i] if i < KEEP else xh[side, 0])
+            y_part = y_part - weight * (yr[side, i] if i < KEEP else yh[side, 0])
+        x_part = x_part * inverse
+        y_part = y_part * inverse
+        z_part = [
+            (zs[1, side, x, :, near_lane:near_lane + 1] * scale
+             - jnp.sum(zh[side, x] * t_row, axis=1, keepdims=True)) * inverse
+            for x in range(bx)]
+        sides.append((x_part, [y_part[x:x + 1] for x in range(bx)], z_part))
+    second = stencil(newest, sides[0][0], sides[1][0], sides[0][1], sides[1][1],
+                     sides[0][2], sides[1][2])
+    for x in range(bx):
+        image[1, x] = second[x]
+    halo_p = field_copies(2, image.at[1])
+    halo_start(halo_p)
+    gram = widen(gram, count, t_row, first_row, length_sq, inverse)
+
+    count = KEEP + 2
+    grown = ufields + [of(abuf), of(image, 1)]
+    p_row = (as_row(dots(second, basis_fields[:count]))
+             + as_row(dots(second, grown), 32))
+    q_row = as_row(dots(newest, grown[:KEEP + 1]), 32)
+    halo_wait(halo_p)
+    third = stencil(
+        second, xs[2, 0], xs[2, 1],
+        [ys[2, 0, x, by - 1:by, :] for x in range(bx)],
+        [ys[2, 1, x, 0:1, :] for x in range(bx)],
+        [zs[2, 0, x, :, bz - 1:bz] for x in range(bx)],
+        [zs[2, 1, x, :, 0:1] for x in range(bx)],
+    )
+    r_row = (as_row(dots(third, basis_fields[:count]))
+             + as_row(dots(third, grown + [lambda x: third[x]]), 32))
+    last = jnp.concatenate([p_row, r_row, q_row], axis=0)
+    earlier = pending[:]
+    pending.clear()
+    last_arrival = total_start(2, last)
+    for copy in earlier:
+        copy.wait()
+    for copies in (halo_w, halo_r, halo_a, halo_p):
+        halo_finish(copies)
+    mixed = total_end(1, mixed, mix_arrival)
+    parts = [jnp.where(lane8 < KEEP,
+                       mixed if k == 0 else pltpu.roll(mixed, LANES - KEEP * k, 1), 0.0)
+             for k in range(6)]
+    across = jnp.concatenate(parts[0:3], axis=0)
+    inside = jnp.concatenate(parts[3:6], axis=0)
+    image_row = across[KEEP + 1:KEEP + 2] * scale
+    across = jnp.where(row < KEEP, across, jnp.where(row == KEEP, across * scale, 0.0))
+    across = jnp.where((lane == KEEP) & (row <= KEEP), as_col(first_row), across)
+    inside = inside * jnp.where(row // 8 > lane // 8, 2.0, 1.0)
+    inside = jnp.where(row == KEEP, jnp.where(lane == KEEP, image_sq, 2.0 * image_row), inside)
+
+    last = total_end(2, last, last_arrival)
+    shifted_last = pltpu.roll(last, LANES - 32, 1)
+    c_row = jnp.where(lane1 < count, last[0:1], 0.0)
+    pz_row = jnp.where(lane1 < count, shifted_last[0:1], 0.0)
+    rq_row = jnp.where(lane1 < count, last[1:2], 0.0)
+    rz_row = jnp.where(lane1 <= count, shifted_last[1:2], 0.0)
+    qz_row = jnp.where(lane1 < KEEP + 1, shifted_last[2:3], 0.0)
+    across = jnp.where(row == KEEP + 1, qz_row, across)
+    across = jnp.where((lane == KEEP + 1) & (row < count), as_col(c_row), across)
+    inside = jnp.where(row == KEEP + 1,
+                       jnp.where(lane == KEEP + 1, pz_row, 2.0 * pz_row), inside)
+    t_row, t_col, weights, length_sq, inverse = step(
+        count, c_row, None, pick(pz_row, KEEP + 1), gram)
+    gram = widen(gram, count, t_row, c_row, length_sq, inverse)
+    h_col = jnp.sum(jnp.where(row == lane, rq_row, 0.0) - across * t_row, axis=1, keepdims=True)
+    th = jnp.sum(t_col * h_col, axis=0, keepdims=True)
+    corner = jnp.sum(jnp.where(lane1 == KEEP + 1, rz_row, 0.0) - pz_row * t_row,
+                     axis=1, keepdims=True)
+    corner = (corner - th) * inverse * inverse
+    wt_row = jnp.sum(inside * t_col, axis=0, keepdims=True)
+    image_sq = jnp.sum(
+        jnp.where(lane1 == count, rz_row, (wt_row - 2.0 * rz_row) * t_row),
+        axis=1, keepdims=True) * inverse * inverse
+    c_col = jnp.where(row1 < count, h_col * inverse, jnp.where(row1 == count, corner, 0.0))
+    newest = [tile * inverse for tile in less(second, weights, basis_fields[:count])]
+    for x in range(bx):
+        out[count, x] = newest[x]
+    applied = [tile * inverse for tile in less(third, weights, grown)]
+    count = KEEP + 3
+    t_row, t_col, weights, length_sq, inverse = step(count, as_row(c_col), c_col, image_sq, gram)
+    newest = [tile * inverse for tile in less(applied, weights, basis_fields[:count])]
+    for x in range(bx):
+        out[count, x] = newest[x]
 
     for k in range(EXPAND):
-        hess[k:k + 1] = hcols[k % len(hcols)]
-    for copies in done:
-        halo_finish(copies)
+        hess[k:k + 1] = hcols[k]
     finish_sends()
 
 
@@ -433,13 +540,13 @@
             pltpu.VMEM((2, 3, LANES), f32),
             pltpu.VMEM((n0 - 1, 3, LANES), f32),
             pltpu.VMEM((nline - 1, 3, LANES), f32),
-            pltpu.VMEM((EXPAND, 1, LANES), f32),
-            pltpu.VMEM((EXPAND, nrow - 1, 1, LANES), f32),
-            pltpu.VMEM((EXPAND, n1 - 1, 1, LANES), f32),
-            pltpu.VMEM((EXPAND, 1, LANES), f32),
+            *[pltpu.VMEM(shape, f32) for rows in (1, 8, 3) for shape in (
+                (rows, LANES), (nrow - 1, rows, LANES), (rows, LANES), (n1 - 1, rows, LANES))],
+            pltpu.VMEM((KEEP,) + block, f32),
+            pltpu.VMEM(block, f32),
             dma((5,)), dma((24,)), dma((24,)),
             dma, dma, dma, dma,
-            dma((EXPAND,)), dma((EXPAND,)), dma((EXPAND,)), dma((EXPAND,)),
+            dma((3, 4)),
             pltpu.SemaphoreType.REGULAR,
         ],
         compiler_params=pltpu.CompilerParams(collective_id=0, has_side_effects=True),

time: 26.5 us -> 25.6 us (0.966)
  Pallas kernels: 24.4 us -> 23.5 us
    pallas_call x1, Pallas kernels: 24.4 us -> 23.5 us  [per_device(): pl.pallas_call(functools.partial(body, sizes, cells), out_shape=(pltpu.VM...]
where the time goes in v1:
time: 25.6 us; the launch traced here: 25.5 us
  Pallas kernels  23.5 us (92%)
  local copies, waits for them, and re-layouts  1.33 us (5%)
  between operations  0.64 us (2%)
    pallas_call x1, Pallas kernels, per_device(): pl.pallas_call(functools.partial(body, sizes, cells), out_shape=(pltpu.VM...  23.5 us
    unnamed x1, local copies, waits for them, and re-layouts  0.75 us
    transpose x1, local copies, waits for them, and re-layouts, per_device(): return (vectors, columns[0:EXPAND, 0:ROWS].T)  0.58 us

profile of v1, /device:TPU:0, one launch (start us, length us, event | category | flops | bytes accessed | tf_op | source)
XLA Modules:
  0.0 25.5 jit_solution(16539069239526941510)
XLA Ops:
  0.6 23.5 %shard_map.68 = (f32[24,4,8,128]{3,2,1,0:T(8,128)S(1)}, f32[8,128]{1,0:T(8,128)S(1)}) custom-call(f32[60,4,8,128]{3,2,1,0:T(8,128)} %kry_hbm.1, f32[20,60]{1,0:T(8,128)} %bitcast.3, f32[4,8,128]{2,1,0:T(8,128)} %w_hbm.1, f32[4,8,128]{2,1,0:T(8,128)} %diag_hbm.1, f32[3,4,8,128]{3,2,1,0:T(8,128)} %vel_hbm.1), custom_call_target="tpu_custom_call" | custom-call | tf_op jit(solution)/shard_map/pallas_call | solution.py:512
  24.1 0.7 %copy.8 = f32[24,4,8,128]{3,2,1,0:T(8,128)} copy(f32[24,4,8,128]{3,2,1,0:T(8,128)S(1)} %get-tuple-element.6) | data formatting | bytes 786432
  24.9 0.6 %slice_bitcast_fusion = f32[24,3]{0,1:T(4,128)} fusion(f32[8,128]{1,0:T(8,128)S(1)} %get-tuple-element.5), kind=kLoop, calls=%fused_computation | loop fusion | bytes 576 | tf_op jit(solution)/shard_map/transpose | solution.py:554

commit v2 on v1

--- a/solution.py
+++ b/solution.py
@@ -1,4 +1,5 @@
 import functools
+import math
 
 import jax
 import jax.numpy as jnp
@@ -11,9 +12,15 @@
 EXPAND = 3
 ROWS = 24
 LANES = 128
-UNIT = 16
 DIRECT = 64
+CHUNK = 5
+MIX = 1
+NEAR = 2
 AXES = ("gx", "gy", "gz")
+
+
+def turns_of(line):
+    return -(-max(line - 2, 0) // NEAR) + 1 if line > 1 else 0
 
 
 def partner_steps(phase, sizes):
@@ -28,19 +35,19 @@
     sizes, cells,
     kry_hbm, schur_hbm, w_hbm, diag_hbm, vel_hbm,
     out, hess,
-    schur, w_ref, diag, vel, kry, image, xr, yr, zr, ypack, zpack, xh, yh, zh, xs, ys, zs,
-    gsend, grecv0, grecv1,
+    schur, w_ref, diag, vel, kry, image, xr, yr, zr, ypack, zpack, xh, yh, zh, yhpack, zhpack, xs, ys, zs,
     rsend, rrecv0, rmid, rrecv1, msend, mrecv0, mmid, mrecv1, lsend, lrecv0, lmid, lrecv1,
-    ubuf, abuf,
-    load_sem, halo_send, halo_recv, gsem_s0, gsem_r0, gsem_s1, gsem_r1, sums_sem, ready,
+    ubuf, abuf, pbuf,
+    load_sem, halo_send, halo_recv, sums_sem, line_sem, ready,
 ):
     place = tuple(lax.axis_index(a) for a in AXES)
-    basis = kry.shape[0]
+    basis = kry_hbm.shape[0]
     bx, by, bz = w_ref.shape
     loads = [
         pltpu.make_async_copy(source, target, load_sem.at[k])
         for k, (source, target) in enumerate((
-            (w_hbm, w_ref), (schur_hbm, schur), (kry_hbm, kry), (diag_hbm, diag), (vel_hbm, vel)))
+            (w_hbm, w_ref), (schur_hbm, schur), (kry_hbm, kry.at[0:basis]), (diag_hbm, diag),
+            (vel_hbm, vel)))
     ]
     for copy in loads:
         copy.start()
@@ -52,50 +59,81 @@
                 for step in partner_steps(phase, sizes)]
 
 
-    for ref in (xr, yr, zr, xs, ys, zs):
+    for ref in (xr, yr, zr, xh, yh, zh, xs, ys, zs):
         ref[...] = jnp.zeros_like(ref)
 
     barrier = pltpu.get_barrier_semaphore()
-    for to in partners(0) + partners(1):
+    line = [
+        ((place[0] + step,) + place[1:],
+         place[0] < sizes[0] - step if step > 0 else place[0] >= -step)
+        for far in range(1, min(NEAR, sizes[0] - 1) + 1) for step in (far, -far)]
+
+    def tell(semaphore, to):
         pl.semaphore_signal(
-            barrier, inc=1, device_id=to, device_id_type=pl.DeviceIdType.MESH)
-    pl.semaphore_wait(barrier, len(partners(0)) + len(partners(1)))
-
-    def halo_copies(kind, sources, targets):
-        found = []
-        for d in range(3):
+            semaphore, inc=1, device_id=to, device_id_type=pl.DeviceIdType.MESH)
+
+    for to in partners(0) + ([] if direct else partners(1)):
+        tell(barrier, to)
+    if direct:
+        for to, near in line:
+            pl.when(near)(functools.partial(tell, barrier, to))
+    turns_needed = turns_of(sizes[0]) if direct else 0
+
+    def pass_on(turn):
+        if 0 < turn <= turns_needed:
+            for side, (to, near) in enumerate(line if turn < turns_needed else line[:2]):
+                pl.when(near)(functools.partial(pl.semaphore_wait, ready.at[turn - 1, side], 1))
+        if turn < turns_needed:
+            for side, (to, near) in enumerate(line if turn + 1 < turns_needed else line[:2]):
+                pl.when(near)(functools.partial(tell, ready.at[turn, side ^ 1], to))
+
+
+    sent = [[] for _ in range(3)]
+
+    def halo_start(kind, dims, sources, targets):
+        for d in dims:
             for side in (0, 1):
-                at = (kind * 3 + d) * 2 + side
                 to = list(place)
                 to[d] = place[d] + (1 if side == 0 else -1)
                 can_send = place[d] < sizes[d] - 1 if side == 0 else place[d] > 0
-                can_recv = place[d] > 0 if side == 0 else place[d] < sizes[d] - 1
-                found.append((
-                    pltpu.make_async_remote_copy(
-                        src_ref=sources[d][side], dst_ref=targets[d][side],
-                        send_sem=halo_send.at[at], recv_sem=halo_recv.at[at],
-                        device_id=tuple(to), device_id_type=pl.DeviceIdType.MESH,
-                    ), can_send, can_recv))
-        return found
-
-    def halo_start(copies):
-        for copy, can_send, _ in copies:
-            pl.when(can_send)(copy.start)
-
-    def halo_wait(copies):
-        for copy, _, can_recv in copies:
-            pl.when(can_recv)(copy.wait_recv)
-
-    def halo_finish(copies):
-        for copy, can_send, _ in copies:
-            pl.when(can_send)(copy.wait_send)
-
-    def field_copies(kind, ref):
-        return halo_copies(
-            kind,
-            ((ref.at[bx - 1], ref.at[0]), (ref, ref), (ref, ref)),
-            tuple((r.at[kind, 0], r.at[kind, 1]) for r in (xs, ys, zs)),
-        )
+                source = sources[d][side]
+                sent[d].append(math.prod(source.shape))
+                pl.when(can_send)(pltpu.make_async_remote_copy(
+                    src_ref=source, dst_ref=targets[d][side],
+                    send_sem=halo_send.at[d], recv_sem=halo_recv.at[kind, d],
+                    device_id=tuple(to), device_id_type=pl.DeviceIdType.MESH).start)
+
+    def landed(ref, semaphore):
+        pltpu.make_async_copy(ref, ref, semaphore).wait()
+
+    def halo_wait(kind, targets):
+        for d in range(3):
+            before, after = place[d] > 0, place[d] < sizes[d] - 1
+            semaphore = halo_recv.at[kind, d]
+            if sizes[d] > 2:
+                pl.when(before & after)(functools.partial(landed, targets[d], semaphore))
+                pl.when(before != after)(functools.partial(landed, targets[d].at[0], semaphore))
+            elif sizes[d] == 2:
+                landed(targets[d].at[0], semaphore)
+
+    def halo_finish():
+        for d in range(3):
+            before, after = place[d] > 0, place[d] < sizes[d] - 1
+            tiles = sum(sent[d]) // 2 // (by * bz)
+            if sizes[d] > 2:
+                pl.when(before & after)(functools.partial(
+                    landed, kry.at[0:tiles, 0:2], halo_send.at[d]))
+                pl.when(before != after)(functools.partial(
+                    landed, kry.at[0:tiles, 0], halo_send.at[d]))
+            elif sizes[d] == 2:
+                landed(kry.at[0:tiles, 0], halo_send.at[d])
+
+    def field_targets(kind):
+        return tuple(r.at[kind] for r in (xs, ys, zs))
+
+    def field_start(kind, ref):
+        halo_start(kind, range(3), ((ref.at[bx - 1], ref.at[0]), (ref, ref), (ref, ref)),
+                   tuple((r.at[0], r.at[1]) for r in field_targets(kind)))
 
     def exchange(send, slots, sem_s, sem_r, phase):
         for at, to in enumerate(partners(phase)):
@@ -125,14 +163,16 @@
     def total_start(k, value):
         send, first = groups[k][:2]
         send[...] = value
-        return exchange(send, first, sums_sem.at[k, 0], sums_sem.at[k, 1], 2 if direct else 0)
+        return exchange(send, first, sums_sem.at[2 * k], sums_sem.at[2 * k + 1],
+                        2 if direct and k != MIX else 0)
 
     def total_end(k, value, arrival):
         first, between, second = groups[k][1:]
         value = gather_sum(arrival, value, first)
-        if not direct:
+        if not direct or k == MIX:
+            at = 0 if direct else k
             between[...] = value
-            arrival = exchange(between, second, sums_sem.at[k, 2], sums_sem.at[k, 3], 1)
+            arrival = exchange(between, second, line_sem.at[2 * at], line_sem.at[2 * at + 1], 1)
             value = gather_sum(arrival, value, second)
         return value * (1.0 / cells)
 
@@ -192,52 +232,77 @@
 
     basis_fields = [of(out, i) for i in range(ROWS)]
 
-    halo_w = field_copies(0, w_ref)
     loads[0].wait()
-    halo_start(halo_w)
-    if direct:
-        for to in partners(1):
-            pl.semaphore_signal(
-                ready, inc=1, device_id=to, device_id_type=pl.DeviceIdType.MESH)
 
     out[KEEP + 1:ROWS] = jnp.zeros((ROWS - KEEP - 1, bx, by, bz), jnp.float32)
     out[KEEP] = w_ref[...]
+    deep = kry.shape[0]
+    for i in range(basis, deep):
+        kry[i] = jnp.zeros((bx, by, bz), jnp.float32)
     loads[1].wait()
+
+    def halves(value):
+        high = value.astype(jnp.bfloat16).astype(jnp.float32)
+        return high, value - high
+
+    def times(a, b):
+        return lax.dot_general(a, b, (((1,), (0,)), ((), ())),
+                               precision=lax.Precision.DEFAULT,
+                               preferred_element_type=jnp.float32)
+
+    spread = (lax.broadcasted_iota(jnp.int32, (basis, deep * by), 1) // by
+              == lax.broadcasted_iota(jnp.int32, (basis, deep * by), 0)).astype(jnp.float32)
+    same = (lax.broadcasted_iota(jnp.int32, (by, deep * by), 1) % by
+            == lax.broadcasted_iota(jnp.int32, (by, deep * by), 0))
+    turns = []
+    for part in halves(schur[...]):
+        wide = times(part, spread)
+        turns.append(jnp.concatenate(
+            [jnp.where(same, jnp.broadcast_to(wide[j:j + 1], same.shape), 0.0)
+             for j in range(KEEP)], axis=0))
+    both = jnp.concatenate(turns, axis=0)
     loads[2].wait()
-    wide, deep = 5, 4
-    for first in range(0, KEEP, wide):
-        def step(at, sums, first=first):
-            sums = list(sums)
-            for k in range(deep):
-                i = at * deep + k
-                for x in range(bx):
-                    tile = kry[i, x]
-                    for j in range(wide):
-                        sums[j * bx + x] = sums[j * bx + x] + schur[first + j, i] * tile
-            return tuple(sums)
-        sums = lax.fori_loop(
-            0, basis // deep, step,
-            tuple(jnp.zeros((by, bz), jnp.float32) for _ in range(wide * bx)))
-        for j in range(wide):
+    for x in range(0, bx, 2):
+        pair = range(x, min(x + 2, bx))
+        tiles = jnp.concatenate([kry[:, k].reshape(deep * by, bz) for k in pair], axis=1)
+        high, low = halves(tiles)
+        first = times(both, high)
+        found = first[:KEEP * by] + (first[KEEP * by:] + times(turns[0], low))
+        for j in range(KEEP):
+            for k in pair:
+                out[j, k] = found[j * by:(j + 1) * by, (k - x) * bz:(k - x + 1) * bz]
+
+    pl.semaphore_wait(barrier, len(partners(0)) + (
+        sum(near.astype(jnp.int32) for _, near in line) if direct else len(partners(1))))
+    field_start(0, w_ref)
+    pass_on(0)
+
+    def face_start(kind, ref, packs, targets, dims, span):
+        (ys_, zs_), (first, last) = packs, span
+        halo_start(
+            kind, dims,
+            ((ref.at[first:last, bx - 1], ref.at[first:last, 0]), (ys_.at[0], ys_.at[1]),
+             (zs_.at[0], zs_.at[1])),
+            tuple((r.at[0, first:last], r.at[1, first:last]) if d == 0 else (r.at[0], r.at[1])
+                  for d, r in enumerate(targets)))
+
+    def pack_faces(ref, packs):
+        ys_, zs_ = packs
+        for side, (near, edge) in enumerate(((by - 1, bz - 1), (0, 0))):
+            for i in range(KEEP):
+                ys_[side, i] = ref[i, :, near, :]
             for x in range(bx):
-                out[first + j, x] = sums[j * bx + x]
-
-    for side, (near, edge) in enumerate(((by - 1, bz - 1), (0, 0))):
-        for i in range(KEEP):
-            ypack[side, i] = out[i, :, near, :]
-        for x in range(bx):
-            face = jnp.zeros((by, bz), jnp.float32)
-            for i in range(KEEP):
-                face = jnp.where(
-                    lane3 == i, pltpu.roll(out[i, x], (i - edge) % bz, 1), face)
-            zpack[side, x] = face
-    halo_r = halo_copies(
-        3,
-        ((out.at[0:KEEP, bx - 1], out.at[0:KEEP, 0]), (ypack.at[0], ypack.at[1]),
-         (zpack.at[0], zpack.at[1])),
-        tuple((r.at[0], r.at[1]) for r in (xr, yr, zr)),
-    )
-    halo_start(halo_r)
+                face = jnp.zeros((by, bz), jnp.float32)
+                for i in range(KEEP):
+                    face = jnp.where(
+                        lane3 == i, pltpu.roll(ref[i, x], (i - edge) % bz, 1), face)
+                zs_[side, x] = face
+
+    turned = (3, out, (ypack, zpack), (xr, yr, zr))
+    face_start(*turned, (0,), (0, KEEP))
+    pack_faces(out, (ypack, zpack))
+    face_start(*turned, (1, 2), (0, KEEP))
+    pass_on(1)
 
     row = lax.broadcasted_iota(jnp.int32, (ROWS, LANES), 0)
     lane = lax.broadcasted_iota(jnp.int32, (ROWS, LANES), 1)
@@ -256,30 +321,13 @@
                    [None] * (j // 8 * 8) + basis_fields[j // 8 * 8:KEEP + 1])
         gram = jnp.where((lane == j) & (row < KEEP + 1), col, gram)
     lane8 = lax.broadcasted_iota(jnp.int32, (8, LANES), 1)
-    own8 = lane8 // UNIT == lax.broadcasted_iota(jnp.int32, (8, LANES), 0)
-
-    def spread(value):
-        for shift in (UNIT, 2 * UNIT, 4 * UNIT):
-            value = value + pltpu.roll(value, shift, 1)
-        return value
-
-    units = (
-        gram[16:24],
-        gram[8:16],
-        jnp.where(lane8 < 8, gram[0:8], pltpu.roll(gram[16:24], LANES - 8, 1)),
-    )
-    packed = jnp.concatenate([
-        jnp.sum(jnp.where(own8, spread(jnp.where(lane8 < UNIT, unit, 0.0)), 0.0),
-                axis=0, keepdims=True)
-        for unit in units], axis=0)
-    gsend[0] = packed
-    if direct:
-        pl.semaphore_wait(ready, sizes[0] - 1)
-    arrival0 = exchange(gsend.at[0], grecv1, gsem_s1, gsem_r1, 2 if direct else 1)
+    below = jnp.where(row // 8 > lane // 8, gram, 0.0)
+    gram = gram + jnp.concatenate(
+        [below, jnp.zeros((LANES - ROWS, LANES), jnp.float32)], axis=0).T[0:ROWS]
 
     loads[3].wait()
     loads[4].wait()
-    halo_wait(halo_w)
+    halo_wait(0, field_targets(0))
     applied = stencil(
         [w_ref[x] for x in range(bx)], xs[0, 0], xs[0, 1],
         [ys[0, 0, x, by - 1:by, :] for x in range(bx)],
@@ -289,12 +337,22 @@
     )
     for x in range(bx):
         image[0, x] = applied[x]
-    ownrow = as_row(dots(applied, basis_fields[:KEEP + 1] + [None, None, of(image, 0)]))
-    row_arrival = total_start(0, ownrow)
-    halo_a = field_copies(1, image.at[0])
-    halo_start(halo_a)
-
-    halo_wait(halo_r)
+    field_start(1, image.at[0])
+    own_sq = jnp.sum(jnp.where((row == KEEP) & (lane == KEEP), gram, 0.0),
+                     axis=0, keepdims=True)
+    own_sq = jnp.sum(own_sq, axis=1, keepdims=True)
+    own = dots(applied, basis_fields[:KEEP + 1] + [None, None, of(image, 0)])
+    own = jnp.where(row1 == KEEP + 1, own_sq, own)
+    gram = jnp.where(lane < KEEP, gram, jnp.where(lane == KEEP, own, 0.0))
+    cut = KEEP + 1
+    packed = gram[0:8] + pltpu.roll(gram[8:16], cut, 1) + pltpu.roll(gram[16:24], 2 * cut, 1)
+    packed = packed[0:4] + pltpu.roll(packed[4:8], 3 * cut, 1)
+    for turn in range(2, turns_needed + 1):
+        pass_on(turn)
+    first_arrival = total_start(0, packed)
+
+    halo_wait(3, (xr, yr, zr))
+    applied_faces = (4, ubuf, (yhpack, zhpack), (xh, yh, zh))
     for i in range(KEEP):
         found = stencil(
             [out[i, x] for x in range(bx)], xr[0, i], xr[1, i],
@@ -302,6 +360,10 @@
             [zr[0, x, :, i:i + 1] for x in range(bx)], [zr[1, x, :, i:i + 1] for x in range(bx)])
         for x in range(bx):
             ubuf[i, x] = found[x]
+        if (i + 1) % CHUNK == 0:
+            face_start(*applied_faces, (0,), (i + 1 - CHUNK, i + 1))
+    pack_faces(ubuf, (yhpack, zhpack))
+    face_start(*applied_faces, (1, 2), (0, KEEP))
     ufields = [of(ubuf, i) for i in range(KEEP)]
     shares = [jnp.zeros((ROWS, LANES), jnp.float32) for _ in range(2)]
     for j in range(KEEP):
@@ -314,44 +376,37 @@
         part = shares[k // 3][k % 3 * 8:k % 3 * 8 + 8]
         mixed = mixed + (part if k == 0 else pltpu.roll(part, KEEP * k, 1))
     mix_arrival = total_start(1, mixed)
-
-    packed = gather_sum(arrival0, packed, grecv1)
-    if not direct:
-        gsend[1] = packed
-        arrival1 = exchange(gsend.at[1], grecv0, gsem_s0, gsem_r0, 0)
-        packed = gather_sum(arrival1, packed, grecv0)
-    packed = packed * (1.0 / cells)
-    units = [
-        jnp.where(lane8 < UNIT,
-                  spread(jnp.where(own8, jnp.broadcast_to(packed[u:u + 1], (8, LANES)), 0.0)),
-                  0.0)
-        for u in range(3)]
-    corner = pltpu.roll(jnp.where(lane8 >= 8, units[2], 0.0), 8, 1)
-    below = jnp.concatenate(
-        [jnp.zeros((8, LANES), jnp.float32), jnp.where(lane8 < 8, units[1], 0.0), units[0],
-         jnp.zeros((LANES - ROWS, LANES), jnp.float32)], axis=0)
+    halo_wait(1, field_targets(1))
+    second = stencil(
+        applied, xs[1, 0], xs[1, 1],
+        [ys[1, 0, x, by - 1:by, :] for x in range(bx)],
+        [ys[1, 1, x, 0:1, :] for x in range(bx)],
+        [zs[1, 0, x, :, bz - 1:bz] for x in range(bx)],
+        [zs[1, 1, x, :, 0:1] for x in range(bx)],
+    )
+    for x in range(bx):
+        image[1, x] = second[x]
+    field_start(2, image.at[1])
+
+    packed = total_end(0, packed, first_arrival)
+    packed = jnp.concatenate([packed, pltpu.roll(packed, LANES - 3 * cut, 1)], axis=0)
     gram = jnp.concatenate(
-        [jnp.where(lane8 < 8, units[2], 0.0), units[1], units[0] + corner], axis=0)
-    gram = gram + below.T[0:ROWS]
-    gram = jnp.where((lane < KEEP + 1) & (row < KEEP + 1), gram, 0.0)
-    norm_sq = jnp.sum(
-        jnp.sum(jnp.where((lane == KEEP) & (row == KEEP), gram, 0.0), axis=1, keepdims=True),
-        axis=0, keepdims=True)
+        [packed, pltpu.roll(packed, LANES - cut, 1), pltpu.roll(packed, LANES - 2 * cut, 1)],
+        axis=0)
+    own = jnp.sum(jnp.where(lane == KEEP, gram, 0.0), axis=1, keepdims=True)
+    norm_sq = own[KEEP + 1:KEEP + 2]
+    image_sq = own[ROWS - 1:ROWS]
+    gram = jnp.where((lane < KEEP) & (row <= KEEP), gram, 0.0)
+    next_row = gram[KEEP:KEEP + 1]
+    gram = jnp.where(lane == KEEP, as_col(next_row) + jnp.where(row1 == KEEP, norm_sq, 0.0), gram)
     scale = 1.0 / jnp.maximum(jnp.sqrt(norm_sq), 0.5)
     gram = gram * jnp.where(row == KEEP, scale, 1.0) * jnp.where(lane == KEEP, scale, 1.0)
     for x in range(bx):
         out[KEEP, x] = w_ref[x] * scale
     applied = [tile * scale for tile in applied]
-    rowform = total_end(0, ownrow, row_arrival)
-    rowform = rowform * scale * jnp.where((lane1 == KEEP) | (lane1 == ROWS - 1), scale, 1.0)
-
-    for side in (0, 1):
-        near_row, near_lane = (by - 1, bz - 1) if side == 0 else (0, 0)
-        xh[side, 0] = xs[0, side] * scale
-        for x in range(bx):
-            yh[side, 0, x:x + 1] = ys[0, side, x, near_row:near_row + 1, :] * scale
-            zh[side, x] = jnp.where(
-                lane3 == KEEP, zs[0, side, x, :, near_lane:near_lane + 1] * scale, zr[side, x])
+    image_sq = image_sq * scale * scale
+    own = jnp.where(row1 <= KEEP, own * scale * jnp.where(row1 == KEEP, scale, 1.0), 0.0)
+
     for x in range(bx):
         abuf[x] = applied[x]
     hcols = []
@@ -392,51 +447,51 @@
         return jnp.sum(jnp.where(lane1 == at, values, 0.0), axis=1, keepdims=True)
 
     count = KEEP + 1
-    first_row = jnp.where(lane1 < count, rowform, 0.0)
-    image_sq = pick(rowform, ROWS - 1)
-    t_row, t_col, weights, length_sq, inverse = step(count, first_row, None, image_sq, gram)
+    first_row = as_row(own)
+    t_row, t_col, weights, length_sq, inverse = step(count, first_row, own, image_sq, gram)
     newest = [tile * inverse for tile in less(applied, weights, basis_fields[:count])]
     for x in range(bx):
         out[count, x] = newest[x]
-    halo_wait(halo_a)
+    second = [tile * inverse for tile in less(
+        [image[1, x] * scale for x in range(bx)], weights, ufields + [of(abuf)])]
+    for x in range(bx):
+        pbuf[x] = second[x]
+    halo_wait(4, (xh, yh, zh))
+    halo_wait(2, field_targets(2))
     sides = []
     for side in (0, 1):
         near_row, near_lane = (by - 1, bz - 1) if side == 0 else (0, 0)
-        x_part = xs[1, side] * scale
-        y_part = [ys[1, side, x, near_row:near_row + 1, :] * scale for x in range(bx)]
-        y_part = jnp.concatenate(y_part, axis=0)
-        for i in range(count):
+
+        def edge(kind):
+            return jnp.concatenate(
+                [ys[kind, side, x, near_row:near_row + 1, :] for x in range(bx)], axis=0)
+
+        weight = weights[KEEP:KEEP + 1, :]
+        x_part = (xs[2, side] - weight * xs[1, side]) * scale
+        y_part = (edge(2) - weight * edge(1)) * scale
+        for i in range(KEEP):
             weight = weights[i:i + 1, :]
-            x_part = x_part - weight * (xr[side, i] if i < KEEP else xh[side, 0])
-            y_part = y_part - weight * (yr[side, i] if i < KEEP else yh[side, 0])
+            x_part = x_part - weight * xh[side, i]
+            y_part = y_part - weight * yh[side, i]
         x_part = x_part * inverse
         y_part = y_part * inverse
-        z_part = [
-            (zs[1, side, x, :, near_lane:near_lane + 1] * scale
-             - jnp.sum(zh[side, x] * t_row, axis=1, keepdims=True)) * inverse
-            for x in range(bx)]
+        z_part = []
+        for x in range(bx):
+            image_edge, own_edge = (
+                zs[kind, side, x, :, near_lane:near_lane + 1] * scale for kind in (2, 1))
+            mine = jnp.where(lane3 == KEEP, own_edge, zh[side, x])
+            z_part.append(
+                (image_edge - jnp.sum(mine * t_row, axis=1, keepdims=True)) * inverse)
         sides.append((x_part, [y_part[x:x + 1] for x in range(bx)], z_part))
-    second = stencil(newest, sides[0][0], sides[1][0], sides[0][1], sides[1][1],
-                     sides[0][2], sides[1][2])
-    for x in range(bx):
-        image[1, x] = second[x]
-    halo_p = field_copies(2, image.at[1])
-    halo_start(halo_p)
     gram = widen(gram, count, t_row, first_row, length_sq, inverse)
 
     count = KEEP + 2
-    grown = ufields + [of(abuf), of(image, 1)]
+    grown = ufields + [of(abuf), of(pbuf)]
     p_row = (as_row(dots(second, basis_fields[:count]))
              + as_row(dots(second, grown), 32))
     q_row = as_row(dots(newest, grown[:KEEP + 1]), 32)
-    halo_wait(halo_p)
-    third = stencil(
-        second, xs[2, 0], xs[2, 1],
-        [ys[2, 0, x, by - 1:by, :] for x in range(bx)],
-        [ys[2, 1, x, 0:1, :] for x in range(bx)],
-        [zs[2, 0, x, :, bz - 1:bz] for x in range(bx)],
-        [zs[2, 1, x, :, 0:1] for x in range(bx)],
-    )
+    third = stencil(second, sides[0][0], sides[1][0], sides[0][1], sides[1][1],
+                    sides[0][2], sides[1][2])
     r_row = (as_row(dots(third, basis_fields[:count]))
              + as_row(dots(third, grown + [lambda x: third[x]]), 32))
     last = jnp.concatenate([p_row, r_row, q_row], axis=0)
@@ -445,8 +500,7 @@
     last_arrival = total_start(2, last)
     for copy in earlier:
         copy.wait()
-    for copies in (halo_w, halo_r, halo_a, halo_p):
-        halo_finish(copies)
+    halo_finish()
     mixed = total_end(1, mixed, mix_arrival)
     parts = [jnp.where(lane8 < KEEP,
                        mixed if k == 0 else pltpu.roll(mixed, LANES - KEEP * k, 1), 0.0)
@@ -455,7 +509,7 @@
     inside = jnp.concatenate(parts[3:6], axis=0)
     image_row = across[KEEP + 1:KEEP + 2] * scale
     across = jnp.where(row < KEEP, across, jnp.where(row == KEEP, across * scale, 0.0))
-    across = jnp.where((lane == KEEP) & (row <= KEEP), as_col(first_row), across)
+    across = jnp.where((lane == KEEP) & (row <= KEEP), own, across)
     inside = inside * jnp.where(row // 8 > lane // 8, 2.0, 1.0)
     inside = jnp.where(row == KEEP, jnp.where(lane == KEEP, image_sq, 2.0 * image_row), inside)
 
@@ -505,7 +559,6 @@
     cells = float(bx * by * bz * sizes[0] * sizes[1] * sizes[2])
     n0, n1 = sizes[1] * sizes[2], sizes[0]
     nrow = n0 * n1 if n0 * n1 <= DIRECT else n0
-    nline = n0 * n1 if n0 * n1 <= DIRECT else n1
     f32 = jnp.float32
     vmem = pl.BlockSpec(memory_space=pltpu.VMEM)
     dma = pltpu.SemaphoreType.DMA
@@ -520,34 +573,34 @@
         ],
         out_specs=(vmem, vmem),
         scratch_shapes=[
-            pltpu.SMEM(schur_vectors.shape[::-1], f32),
+            pltpu.VMEM(schur_vectors.shape[::-1], f32),
             pltpu.VMEM(block, f32),
             pltpu.VMEM(block, f32),
             pltpu.VMEM((3,) + block, f32),
-            pltpu.VMEM(krylov_basis.shape, f32),
+            pltpu.VMEM(((krylov_basis.shape[0] + 15) // 16 * 16,) + block, f32),
             pltpu.VMEM((2,) + block, f32),
             pltpu.VMEM((2, KEEP, by, bz), f32),
             pltpu.VMEM((2, KEEP, bx, bz), f32),
             pltpu.VMEM((2,) + block, f32),
             pltpu.VMEM((2, KEEP, bx, bz), f32),
             pltpu.VMEM((2,) + block, f32),
-            pltpu.VMEM((2, EXPAND, by, bz), f32),
-            pltpu.VMEM((2, EXPAND, bx, bz), f32),
+            pltpu.VMEM((2, KEEP, by, bz), f32),
+            pltpu.VMEM((2, KEEP, bx, bz), f32),
+            pltpu.VMEM((2,) + block, f32),
+            pltpu.VMEM((2, KEEP, bx, bz), f32),
             pltpu.VMEM((2,) + block, f32),
             pltpu.VMEM((EXPAND, 2, by, bz), f32),
             pltpu.VMEM((EXPAND, 2) + block, f32),
             pltpu.VMEM((EXPAND, 2) + block, f32),
-            pltpu.VMEM((2, 3, LANES), f32),
-            pltpu.VMEM((n0 - 1, 3, LANES), f32),
-            pltpu.VMEM((nline - 1, 3, LANES), f32),
-            *[pltpu.VMEM(shape, f32) for rows in (1, 8, 3) for shape in (
-                (rows, LANES), (nrow - 1, rows, LANES), (rows, LANES), (n1 - 1, rows, LANES))],
+            *[pltpu.VMEM(shape, f32) for k, rows in enumerate((4, 8, 3)) for shape in (
+                (rows, LANES), ((n0 if k == MIX else nrow) - 1, rows, LANES), (rows, LANES),
+                (n1 - 1, rows, LANES))],
             pltpu.VMEM((KEEP,) + block, f32),
             pltpu.VMEM(block, f32),
-            dma((5,)), dma((24,)), dma((24,)),
-            dma, dma, dma, dma,
-            dma((3, 4)),
-            pltpu.SemaphoreType.REGULAR,
+            pltpu.VMEM(block, f32),
+            dma((5,)), dma((3,)), dma((5, 3)),
+            dma((6,)), dma((2 if nrow > n0 else 6,)),
+            pltpu.SemaphoreType.REGULAR((max(turns_of(sizes[0]), 1), 2 * NEAR)),
         ],
         compiler_params=pltpu.CompilerParams(collective_id=0, has_side_effects=True),
     )(krylov_basis, schur_vectors.T, next_vector, diag_shift, velocity)

time: 25.6 us -> 22.5 us (0.88)
  Pallas kernels: 23.5 us -> 20.3 us
    pallas_call x1, Pallas kernels: 23.5 us -> 20.3 us  [per_device(): pl.pallas_call(functools.partial(body, sizes, cells), out_shape=(pltpu.VM...]
where the time goes in v2:
time: 22.5 us; the launch traced here: 22.3 us
  Pallas kernels  20.3 us (90%)
  local copies, waits for them, and re-layouts  1.33 us (6%)
  between operations  0.64 us (3%)
    pallas_call x1, Pallas kernels, per_device(): pl.pallas_call(functools.partial(body, sizes, cells), out_shape=(pltpu.VM...  20.3 us
    unnamed x1, local copies, waits for them, and re-layouts  0.75 us
    transpose x1, local copies, waits for them, and re-layouts, per_device(): return (vectors, columns[0:EXPAND, 0:ROWS].T)  0.58 us

profile of v2, /device:TPU:0, one launch (start us, length us, event | category | flops | bytes accessed | tf_op | source)
XLA Modules:
  0.0 22.3 jit_solution(2217919120534911669)
XLA Ops:
  0.6 20.3 %shard_map.68 = (f32[24,4,8,128]{3,2,1,0:T(8,128)S(1)}, f32[8,128]{1,0:T(8,128)S(1)}) custom-call(f32[60,4,8,128]{3,2,1,0:T(8,128)} %kry_hbm.1, f32[20,60]{1,0:T(8,128)} %bitcast.3, f32[4,8,128]{2,1,0:T(8,128)} %w_hbm.1, f32[4,8,128]{2,1,0:T(8,128)} %diag_hbm.1, f32[3,4,8,128]{3,2,1,0:T(8,128)} %vel_hbm.1), custom_call_target="tpu_custom_call" | custom-call | tf_op jit(solution)/shard_map/pallas_call | solution.py:565
  21.0 0.7 %copy.8 = f32[24,4,8,128]{3,2,1,0:T(8,128)} copy(f32[24,4,8,128]{3,2,1,0:T(8,128)S(1)} %get-tuple-element.6) | data formatting | bytes 786432
  21.7 0.6 %slice_bitcast_fusion = f32[24,3]{0,1:T(4,128)} fusion(f32[8,128]{1,0:T(8,128)S(1)} %get-tuple-element.5), kind=kLoop, calls=%fused_computation | loop fusion | bytes 576 | tf_op jit(solution)/shard_map/transpose | solution.py:607

commit v3 on v2

--- a/solution.py
+++ b/solution.py
@@ -365,17 +365,14 @@
     pack_faces(ubuf, (yhpack, zhpack))
     face_start(*applied_faces, (1, 2), (0, KEEP))
     ufields = [of(ubuf, i) for i in range(KEEP)]
-    shares = [jnp.zeros((ROWS, LANES), jnp.float32) for _ in range(2)]
-    for j in range(KEEP):
-        v = [ubuf[j, x] for x in range(bx)]
-        cols = (dots(v, basis_fields[:KEEP] + [of(w_ref), of(image, 0)]),
-                dots(v, [None] * (j // 8 * 8) + ufields[j // 8 * 8:]))
-        shares = [jnp.where(lane == j, col, part) for col, part in zip(cols, shares)]
-    mixed = jnp.zeros((8, LANES), jnp.float32)
-    for k in range(6):
-        part = shares[k // 3][k % 3 * 8:k % 3 * 8 + 8]
-        mixed = mixed + (part if k == 0 else pltpu.roll(part, KEEP * k, 1))
-    mix_arrival = total_start(1, mixed)
+    def table(fields):
+        part = jnp.zeros((ROWS, LANES), jnp.float32)
+        for j in range(KEEP):
+            part = jnp.where(
+                lane == j, dots([ubuf[j, x] for x in range(bx)], fields(j)), part)
+        return part
+
+    shares = [table(lambda j: basis_fields[:KEEP] + [of(w_ref), of(image, 0)])]
     halo_wait(1, field_targets(1))
     second = stencil(
         applied, xs[1, 0], xs[1, 1],
@@ -388,6 +385,12 @@
         image[1, x] = second[x]
     field_start(2, image.at[1])
 
+    shares.append(table(lambda j: [None] * (j // 8 * 8) + ufields[j // 8 * 8:]))
+    mixed = jnp.zeros((8, LANES), jnp.float32)
+    for k in range(6):
+        part = shares[k // 3][k % 3 * 8:k % 3 * 8 + 8]
+        mixed = mixed + (part if k == 0 else pltpu.roll(part, KEEP * k, 1))
+    mix_arrival = total_start(1, mixed)
     packed = total_end(0, packed, first_arrival)
     packed = jnp.concatenate([packed, pltpu.roll(packed, LANES - 3 * cut, 1)], axis=0)
     gram = jnp.concatenate(
@@ -548,8 +551,18 @@
         out[count, x] = newest[x]
 
     for k in range(EXPAND):
-        hess[k:k + 1] = hcols[k]
+        hess[k:k + 1] = hcols[k][:, 0:ROWS]
     finish_sends()
+
+
+def hand_out(vectors, columns, vectors_hbm, columns_hbm, semaphores):
+    copies = [
+        pltpu.make_async_copy(source, target, semaphores.at[k])
+        for k, (source, target) in enumerate(((vectors, vectors_hbm), (columns, columns_hbm)))]
+    for copy in copies:
+        copy.start()
+    for copy in copies:
+        copy.wait()
 
 
 def per_device(krylov_basis, schur_vectors, next_vector, diag_shift, velocity):
@@ -566,7 +579,7 @@
         functools.partial(body, sizes, cells),
         out_shape=(
             pltpu.VMEM((ROWS,) + block, f32),
-            pltpu.VMEM((8, LANES), f32),
+            pltpu.VMEM((EXPAND, ROWS), f32),
         ),
         in_specs=[
             pl.BlockSpec(memory_space=pl.ANY) for _ in range(5)
@@ -604,7 +617,15 @@
         ],
         compiler_params=pltpu.CompilerParams(collective_id=0, has_side_effects=True),
     )(krylov_basis, schur_vectors.T, next_vector, diag_shift, velocity)
-    return vectors, columns[0:EXPAND, 0:ROWS].T
+    results = [pltpu.with_memory_space_constraint(r, pltpu.VMEM) for r in (vectors, columns)]
+    vectors, columns = pl.pallas_call(
+        hand_out,
+        out_shape=[jax.ShapeDtypeStruct(r.shape, f32) for r in results],
+        in_specs=[vmem, vmem],
+        out_specs=[pl.BlockSpec(memory_space=pl.ANY)] * 2,
+        scratch_shapes=[dma((2,))],
+    )(*results)
+    return vectors, columns.T
 
 
 def solution(mesh):

time: 22.5 us -> 21.7 us (0.964)
  local copies, waits for them, and re-layouts: 1.33 us -> 0 us
  Pallas kernels: 20.3 us -> 20.8 us
    pallas_call x0 -> x1, Pallas kernels: none -> 0.77 us  [per_device(): pl.pallas_call(hand_out, out_shape=[jax.ShapeDtypeStruct(r.shape, f32) fo...]
    unnamed x1 -> x0, local copies, waits for them, and re-layouts: 0.75 us -> none
    transpose x1 -> x0, local copies, waits for them, and re-layouts: 0.58 us -> none  [per_device(): return (vectors, columns[0:EXPAND, 0:ROWS].T)]
    pallas_call x1, Pallas kernels: 20.3 us -> 20.1 us  [per_device(): pl.pallas_call(functools.partial(body, sizes, cells), out_shape=(pltpu.VM...]
where the time goes in v3:
time: 21.7 us; the launch traced here: 21.5 us
  Pallas kernels  20.8 us (96%)
  between operations  0.64 us (3%)
    pallas_call x1, Pallas kernels, per_device(): pl.pallas_call(functools.partial(body, sizes, cells), out_shape=(pltpu.VM...  20.1 us
    pallas_call x1, Pallas kernels, per_device(): pl.pallas_call(hand_out, out_shape=[jax.ShapeDtypeStruct(r.shape, f32) fo...  0.77 us

profile of v3, /device:TPU:0, one launch (start us, length us, event | category | flops | bytes accessed | tf_op | source)
XLA Modules:
  0.0 21.5 jit_solution(16811768814706628734)
XLA Ops:
  0.6 20.1 %shard_map.68 = (f32[24,4,8,128]{3,2,1,0:T(8,128)S(1)}, f32[3,24]{1,0:T(4,128)S(1)}) custom-call(f32[60,4,8,128]{3,2,1,0:T(8,128)} %kry_hbm.1, f32[20,60]{1,0:T(8,128)} %bitcast.2, f32[4,8,128]{2,1,0:T(8,128)} %w_hbm.1, f32[4,8,128]{2,1,0:T(8,128)} %diag_hbm.1, f32[3,4,8,128]{3,2,1,0:T(8,128)} %vel_hbm.1), custom_call_target="tpu_custom_call" | custom-call | tf_op jit(solution)/shard_map/pallas_call | solution.py:578
  20.7 0.8 %shard_map.69 = (f32[24,4,8,128]{3,2,1,0:T(8,128)}, f32[3,24]{1,0:T(4,128)}) custom-call(f32[24,4,8,128]{3,2,1,0:T(8,128)S(1)} %get-tuple-element.6.vectors, f32[3,24]{1,0:T(4,128)S(1)} %get-tuple-element.7.columns), custom_call_target="tpu_custom_call" | custom-call | tf_op jit(solution)/shard_map/pallas_call | solution.py:621

commit v4 on v3

--- a/solution.py
+++ b/solution.py
@@ -302,7 +302,6 @@
     face_start(*turned, (0,), (0, KEEP))
     pack_faces(out, (ypack, zpack))
     face_start(*turned, (1, 2), (0, KEEP))
-    pass_on(1)
 
     row = lax.broadcasted_iota(jnp.int32, (ROWS, LANES), 0)
     lane = lax.broadcasted_iota(jnp.int32, (ROWS, LANES), 1)
@@ -325,6 +324,15 @@
     gram = gram + jnp.concatenate(
         [below, jnp.zeros((LANES - ROWS, LANES), jnp.float32)], axis=0).T[0:ROWS]
 
+    own_sq = jnp.sum(jnp.where((row == KEEP) & (lane == KEEP), gram, 0.0),
+                     axis=0, keepdims=True)
+    own_sq = jnp.sum(own_sq, axis=1, keepdims=True)
+    gram = jnp.where(lane < KEEP, gram, 0.0)
+    cut = KEEP + 1
+    packed = gram[0:8] + pltpu.roll(gram[8:16], cut, 1) + pltpu.roll(gram[16:24], 2 * cut, 1)
+    packed = packed[0:4] + pltpu.roll(packed[4:8], 3 * cut, 1)
+    lane4 = lax.broadcasted_iota(jnp.int32, (4, LANES), 1)
+    pass_on(1)
     loads[3].wait()
     loads[4].wait()
     halo_wait(0, field_targets(0))
@@ -338,15 +346,11 @@
     for x in range(bx):
         image[0, x] = applied[x]
     field_start(1, image.at[0])
-    own_sq = jnp.sum(jnp.where((row == KEEP) & (lane == KEEP), gram, 0.0),
-                     axis=0, keepdims=True)
-    own_sq = jnp.sum(own_sq, axis=1, keepdims=True)
     own = dots(applied, basis_fields[:KEEP + 1] + [None, None, of(image, 0)])
     own = jnp.where(row1 == KEEP + 1, own_sq, own)
-    gram = jnp.where(lane < KEEP, gram, jnp.where(lane == KEEP, own, 0.0))
-    cut = KEEP + 1
-    packed = gram[0:8] + pltpu.roll(gram[8:16], cut, 1) + pltpu.roll(gram[16:24], 2 * cut, 1)
-    packed = packed[0:4] + pltpu.roll(packed[4:8], 3 * cut, 1)
+    for k in range(6):
+        packed = jnp.where(lane4 == cut * (k % 2 * 3 + k // 2) + KEEP,
+                           own[4 * k:4 * k + 4], packed)
     for turn in range(2, turns_needed + 1):
         pass_on(turn)
     first_arrival = total_start(0, packed)
@@ -392,16 +396,24 @@
         mixed = mixed + (part if k == 0 else pltpu.roll(part, KEEP * k, 1))
     mix_arrival = total_start(1, mixed)
     packed = total_end(0, packed, first_arrival)
+    def place_of(at):
+        return cut * (at // 4 % 2 * 3 + at // 8)
+
+    again = jnp.concatenate([packed] * (ROWS // 4), axis=0)
+    own = jnp.sum(jnp.where(lane == place_of(row) + KEEP, again, 0.0), axis=1, keepdims=True)
+    norm_sq = own[KEEP + 1:KEEP + 2]
+    image_sq = own[ROWS - 1:ROWS]
+    next_row = packed[KEEP % 4:KEEP % 4 + 1]
+    next_col = jnp.sum(
+        jnp.where((lane == row + place_of(KEEP)) & (row < KEEP), next_row, 0.0),
+        axis=1, keepdims=True)
+    next_col = next_col + jnp.where(row1 == KEEP, norm_sq, 0.0)
     packed = jnp.concatenate([packed, pltpu.roll(packed, LANES - 3 * cut, 1)], axis=0)
     gram = jnp.concatenate(
         [packed, pltpu.roll(packed, LANES - cut, 1), pltpu.roll(packed, LANES - 2 * cut, 1)],
         axis=0)
-    own = jnp.sum(jnp.where(lane == KEEP, gram, 0.0), axis=1, keepdims=True)
-    norm_sq = own[KEEP + 1:KEEP + 2]
-    image_sq = own[ROWS - 1:ROWS]
     gram = jnp.where((lane < KEEP) & (row <= KEEP), gram, 0.0)
-    next_row = gram[KEEP:KEEP + 1]
-    gram = jnp.where(lane == KEEP, as_col(next_row) + jnp.where(row1 == KEEP, norm_sq, 0.0), gram)
+    gram = jnp.where(lane == KEEP, next_col, gram)
     scale = 1.0 / jnp.maximum(jnp.sqrt(norm_sq), 0.5)
     gram = gram * jnp.where(row == KEEP, scale, 1.0) * jnp.where(lane == KEEP, scale, 1.0)
     for x in range(bx):

time: 21.7 us -> 21.7 us (level)
  no operation moved by 1% of the time
where the time goes in v4:
time: 21.7 us; the launch traced here: 21.5 us
  Pallas kernels  20.8 us (96%)
  between operations  0.64 us (3%)
    pallas_call x1, Pallas kernels, per_device(): pl.pallas_call(functools.partial(body, sizes, cells), out_shape=(pltpu.VM...  20.1 us
    pallas_call x1, Pallas kernels, per_device(): pl.pallas_call(hand_out, out_shape=[jax.ShapeDtypeStruct(r.shape, f32) fo...  0.77 us

profile of v4, /device:TPU:0, one launch (start us, length us, event | category | flops | bytes accessed | tf_op | source)
XLA Modules:
  0.0 21.5 jit_solution(15034024717880735441)
XLA Ops:
  0.6 20.1 %shard_map.68 = (f32[24,4,8,128]{3,2,1,0:T(8,128)S(1)}, f32[3,24]{1,0:T(4,128)S(1)}) custom-call(f32[60,4,8,128]{3,2,1,0:T(8,128)} %kry_hbm.1, f32[20,60]{1,0:T(8,128)} %bitcast.2, f32[4,8,128]{2,1,0:T(8,128)} %w_hbm.1, f32[4,8,128]{2,1,0:T(8,128)} %diag_hbm.1, f32[3,4,8,128]{3,2,1,0:T(8,128)} %vel_hbm.1), custom_call_target="tpu_custom_call" | custom-call | tf_op jit(solution)/shard_map/pallas_call | solution.py:590
  20.7 0.8 %shard_map.69 = (f32[24,4,8,128]{3,2,1,0:T(8,128)}, f32[3,24]{1,0:T(4,128)}) custom-call(f32[24,4,8,128]{3,2,1,0:T(8,128)S(1)} %get-tuple-element.6.vectors, f32[3,24]{1,0:T(4,128)S(1)} %get-tuple-element.7.columns), custom_call_target="tpu_custom_call" | custom-call | tf_op jit(solution)/shard_map/pallas_call | solution.py:633

commit v5 on v4

--- a/solution.py
+++ b/solution.py
@@ -16,6 +16,7 @@
 CHUNK = 5
 MIX = 1
 NEAR = 2
+SLOT = (0, 1, 0, 2, 3)
 AXES = ("gx", "gy", "gz")
 
 
@@ -82,10 +83,10 @@
     def pass_on(turn):
         if 0 < turn <= turns_needed:
             for side, (to, near) in enumerate(line if turn < turns_needed else line[:2]):
-                pl.when(near)(functools.partial(pl.semaphore_wait, ready.at[turn - 1, side], 1))
+                pl.when(near)(functools.partial(pl.semaphore_wait, ready.at[2 * NEAR * (turn - 1) + side], 1))
         if turn < turns_needed:
             for side, (to, near) in enumerate(line if turn + 1 < turns_needed else line[:2]):
-                pl.when(near)(functools.partial(tell, ready.at[turn, side ^ 1], to))
+                pl.when(near)(functools.partial(tell, ready.at[2 * NEAR * turn + (side ^ 1)], to))
 
 
     sent = [[] for _ in range(3)]
@@ -100,7 +101,7 @@
                 sent[d].append(math.prod(source.shape))
                 pl.when(can_send)(pltpu.make_async_remote_copy(
                     src_ref=source, dst_ref=targets[d][side],
-                    send_sem=halo_send.at[d], recv_sem=halo_recv.at[kind, d],
+                    send_sem=halo_send.at[d], recv_sem=halo_recv.at[SLOT[kind], d],
                     device_id=tuple(to), device_id_type=pl.DeviceIdType.MESH).start)
 
     def landed(ref, semaphore):
@@ -109,7 +110,7 @@
     def halo_wait(kind, targets):
         for d in range(3):
             before, after = place[d] > 0, place[d] < sizes[d] - 1
-            semaphore = halo_recv.at[kind, d]
+            semaphore = halo_recv.at[SLOT[kind], d]
             if sizes[d] > 2:
                 pl.when(before & after)(functools.partial(landed, targets[d], semaphore))
                 pl.when(before != after)(functools.partial(landed, targets[d].at[0], semaphore))
@@ -623,9 +624,9 @@
             pltpu.VMEM((KEEP,) + block, f32),
             pltpu.VMEM(block, f32),
             pltpu.VMEM(block, f32),
-            dma((5,)), dma((3,)), dma((5, 3)),
+            dma((5,)), dma((3,)), dma((4, 3)),
             dma((6,)), dma((2 if nrow > n0 else 6,)),
-            pltpu.SemaphoreType.REGULAR((max(turns_of(sizes[0]), 1), 2 * NEAR)),
+            pltpu.SemaphoreType.REGULAR((2 * NEAR * max(turns_of(sizes[0]) - 1, 0) + 2,)),
         ],
         compiler_params=pltpu.CompilerParams(collective_id=0, has_side_effects=True),
     )(krylov_basis, schur_vectors.T, next_vector, diag_shift, velocity)

time: 21.7 us -> 21.7 us (level)
  no operation moved by 1% of the time
where the time goes in v5:
time: 21.7 us; the launch traced here: 21.4 us
  Pallas kernels  20.8 us (96%)
  between operations  0.64 us (3%)
    pallas_call x1, Pallas kernels, per_device(): pl.pallas_call(functools.partial(body, sizes, cells), out_shape=(pltpu.VM...  20 us
    pallas_call x1, Pallas kernels, per_device(): pl.pallas_call(hand_out, out_shape=[jax.ShapeDtypeStruct(r.shape, f32) fo...  0.77 us

profile of v5, /device:TPU:0, one launch (start us, length us, event | category | flops | bytes accessed | tf_op | source)
XLA Modules:
  0.0 21.4 jit_solution(10534351102265479721)
XLA Ops:
  0.6 20.0 %shard_map.68 = (f32[24,4,8,128]{3,2,1,0:T(8,128)S(1)}, f32[3,24]{1,0:T(4,128)S(1)}) custom-call(f32[60,4,8,128]{3,2,1,0:T(8,128)} %kry_hbm.1, f32[20,60]{1,0:T(8,128)} %bitcast.2, f32[4,8,128]{2,1,0:T(8,128)} %w_hbm.1, f32[4,8,128]{2,1,0:T(8,128)} %diag_hbm.1, f32[3,4,8,128]{3,2,1,0:T(8,128)} %vel_hbm.1), custom_call_target="tpu_custom_call" | custom-call | tf_op jit(solution)/shard_map/pallas_call | solution.py:591
  20.7 0.8 %shard_map.69 = (f32[24,4,8,128]{3,2,1,0:T(8,128)}, f32[3,24]{1,0:T(4,128)}) custom-call(f32[24,4,8,128]{3,2,1,0:T(8,128)S(1)} %get-tuple-element.6.vectors, f32[3,24]{1,0:T(4,128)S(1)} %get-tuple-element.7.columns), custom_call_target="tpu_custom_call" | custom-call | tf_op jit(solution)/shard_map/pallas_call | solution.py:634
